TPU v7x, 256 devices: a whole 4x4x8 slice. The times are simulated.
256 devices in a mesh: py: 8 (over x, y_lo), px: 32 (over y_hi, z, core).
Axes of the slice: x: 4, y: 4 (y_hi: 2, y_lo: 2; y = y_hi * 2 + y_lo), z: 8, core: 2. Of those that a mesh axis runs over, the one named last changes fastest.
Arguments:
- movie: bfloat16 [512, 512, 2048], P('py', 'px'), may hold values from -6 to 6
- traces: bfloat16 [4096, 2048], P('py', 'px'), may hold values from -0.125 to 0.125
- footprints: float32 [512, 512, 512], P('py', 'px'), may hold values from 0 to 1
- block_ids: int32 [8, 32, 4], P('py', 'px'), may hold values from 0 to 32, as said below
Outputs:
- updated: float32 [512, 512, 512], P('py', 'px')
Inputs may be any that keep to these rules, and one draw needn't show every extreme that they name: `block_ids`: in each tile's list of 4 entries the live entries come first and are distinct block numbers below 32; the remaining entries equal 32 and mark empty slots. Every tile has at least one live entry, and some tile has all 4 live.
All inputs are finite; a program needn't handle non-finite values.
Results may differ from a plain program's by a relative error of at most 0.0003.
Values may be sent and summed in bfloat16 or wider, within the bound.
No kernel may reach another device: no remote copies, remote signals or barrier semaphores. Data moves between devices by JAX's collectives and lax.ppermute only.
A program may use at most 64 MiB of HBM per device.

v0:
```python
import functools

import jax
import jax.numpy as jnp
from jax import lax
from jax.sharding import Mesh
from jax.sharding import PartitionSpec as P

K = 4096
BLK = 128
SLOTS = 4
ITERS = 2
PY = ("py_0", "py_1")
PX = ("px_0", "px_1", "px_2")
PY_PX = ("py_0", "py_1", "px_0", "px_1", "px_2")


def joined_along(pieces, dim):
    pieces = jnp.moveaxis(pieces, 0, dim)
    lengths = pieces.shape
    return pieces.reshape(*lengths[:dim], lengths[dim] * lengths[dim + 1], *lengths[dim + 2 :])


def sent_to_all(value, axis):
    copies = jnp.broadcast_to(value, (lax.axis_size(axis), *value.shape))
    return lax.all_to_all(copies, axis, split_axis=0, concat_axis=0, tiled=True)


def collect(value, axis, dim):
    return joined_along(sent_to_all(value, axis), dim)


def over_axes(value, axes):
    return functools.reduce(lax.psum, axes, value)


def accumulate(tile_movie, picked):
    cross = lax.dot_general(
        tile_movie, picked, (((1,), (1,)), ((), ())), preferred_element_type=jnp.float32
    )
    gram = lax.dot_general(
        picked, picked, (((1,), (1,)), ((), ())), preferred_element_type=jnp.float32
    )
    return (cross, gram)


def per_device(movie, traces, footprints, block_ids):
    rows, cols, frames = movie.shape
    pixels = rows * cols
    width = SLOTS * BLK
    nblk = K // BLK
    tile_movie = movie.reshape(pixels, frames)
    ids = block_ids.reshape(SLOTS)
    onehot = (ids[:, None] == jnp.arange(nblk, dtype=jnp.int32)[None, :]).astype(jnp.float32)
    live = jnp.sum(onehot, axis=1)
    span_all = collect(traces, PY, 0)
    span_len = span_all.shape[1]
    row_ids = collect(block_ids, PX, 1).reshape(-1, SLOTS)
    route = (row_ids[:, :, None] == jnp.arange(nblk, dtype=jnp.int32)[None, None, :]).astype(
        jnp.bfloat16
    )
    outgoing = jnp.einsum(
        "rsb,bnw->rsnw",
        route,
        span_all.reshape(nblk, BLK, span_len),
        preferred_element_type=jnp.float32,
    )
    outgoing = outgoing.astype(jnp.bfloat16).reshape(row_ids.shape[0], width, span_len)
    received = lax.all_to_all(outgoing, PX, split_axis=0, concat_axis=2, tiled=True)
    mine = received.reshape(width, frames)
    cross, gram = accumulate(tile_movie, mine)
    column_live = jnp.repeat(live, BLK)
    denom = jnp.diagonal(gram) + 1e-06 + (1.0 - column_live)
    current = footprints.reshape(pixels, width) * column_live[None, :]
    pixall = pixels * lax.axis_size(PY) * lax.axis_size(PX)
    for step in range(ITERS):
        for slot in range(SLOTS):
            low = slot * BLK
            resid = cross[:, low : low + BLK] - jnp.dot(
                current, gram[:, low : low + BLK], precision=lax.Precision.HIGHEST
            )
            fresh = jnp.maximum(
                current[:, low : low + BLK] + resid / denom[None, low : low + BLK], 0.0
            )
            current = current.at[:, low : low + BLK].set(fresh)
        colsq = jnp.sum(current * current, axis=0).reshape(SLOTS, BLK)
        partial_value = jnp.einsum("sb,sn->bn", onehot, colsq, precision=lax.Precision.HIGHEST)
        totals = over_axes(partial_value, PY_PX)
        factor = 1.0 / jnp.sqrt(totals / pixall + 1e-06)
        scale = jnp.einsum("sb,bn->sn", onehot, factor, precision=lax.Precision.HIGHEST).reshape(
            width
        )
        current = current * scale[None, :]
    return current.reshape(rows, cols, width)


def solution(mesh):
    finer = Mesh(mesh.devices.reshape(4, 2, 2, 8, 2), ("py_0", "py_1", "px_0", "px_1", "px_2"))
    placed = (P(PY, PX, None), P(PY, PX), P(PY, PX, None), P(PY, PX, None))
    return jax.shard_map(
        per_device, mesh=finer, in_specs=placed, out_specs=P(PY, PX, None), check_vma=False
    )
```

profile of v0, /device:TPU:1, one launch (start us, length us, event | category | flops | bytes accessed | tf_op | source)
XLA Modules:
  0.0 266.6 jit_solution(13787179059593425669)
XLA Ops:
  0.0 0.7 broadcast_in_dim.11
  0.7 21.9 %all_to_all.25 = s32[32,1,1,4]{3,2,1,0:T(1,128)S(1)} all-to-all(s32[32,1,1,4]{3,2,1,0:T(1,128)S(1)} %broadcast_in_dim.11), channel_id=1, replica_groups=mesh['py_0'=4,'py_1'=2,'px_0'=2,'px_1'=8,'px_2'=2] {'px_0','px_1','px_2'}, dimensions={0} | all-to-all | bytes 1024 | tf_op jit(solution)/shard_map/all_to_all | solution.py:26
  22.6 1.7 broadcast_in_dim.12
  24.2 4.1 %all-to-all-start.1 = ((bf16[8,512,64]{1,2,0:T(8,128)(2,1)}), bf16[8,512,64]{1,2,0:T(8,128)(2,1)S(1)}, u32[]{:S(2)}, u32[]{:S(2)}) async-start(bf16[8,512,64]{1,2,0:T(8,128)(2,1)} %broadcast_in_dim.12), calls=%async_computation.1 | async-start | bytes 1048576 | tf_op jit(solution)/shard_map/all_to_all | solution.py:26
  28.4 0.1 copy.40
  28.5 8.6 %all-to-all-done.1 = bf16[8,512,64]{1,2,0:T(8,128)(2,1)S(1)} async-done(((bf16[8,512,64]{1,2,0:T(8,128)(2,1)}), bf16[8,512,64]{1,2,0:T(8,128)(2,1)S(1)}, u32[]{:S(2)}, u32[]{:S(2)}) %all-to-all-start.1) | async-done | bytes 524320 | tf_op jit(solution)/shard_map/all_to_all | solution.py:26
  37.1 0.3 copy.41
  37.4 0.3 reshape.239
  37.7 0.8 convolution_convert_fusion
  38.4 1.6 copy.42
  40.1 2.2 reshape.225
  42.3 0.0 copy-start.3
  42.3 6.2 %all-to-all-start.2 = ((bf16[32,512,64]{1,2,0:T(8,128)(2,1)}), bf16[32,512,64]{1,2,0:T(8,128)(2,1)}, u32[]{:S(2)}, u32[]{:S(2)}) async-start(bf16[32,512,64]{1,2,0:T(8,128)(2,1)} %reshape.225), calls=%async_computation.2 | async-start | bytes 4194304 | tf_op jit(solution)/shard_map/all_to_all | solution.py:69
  48.6 0.0 copy-done.3
  48.6 0.0 copy-start.4
  48.6 1.8 copy.39
  50.4 0.6 compare_reduce_fusion.2
  51.0 0.7 compare_reduce_fusion
  51.8 0.0 copy-done.4
  51.8 0.2 convert_reduce_fusion
  52.0 0.1 broadcast_bitcast_fusion
  52.0 1.8 broadcast_multiply_fusion.2
  53.8 45.6 %all-to-all-done.2 = bf16[32,512,64]{1,2,0:T(8,128)(2,1)} async-done(((bf16[32,512,64]{1,2,0:T(8,128)(2,1)}), bf16[32,512,64]{1,2,0:T(8,128)(2,1)}, u32[]{:S(2)}, u32[]{:S(2)}) %all-to-all-start.2) | async-done | bytes 2097184 | tf_op jit(solution)/shard_map/all_to_all | solution.py:69
  99.5 3.5 %fusion.2 = f32[512,512]{1,0:T(8,128)S(1)} fusion(bf16[32,512,64]{1,2,0:T(8,128)(2,1)} %all-to-all-done.2), kind=kOutput, calls=%fused_computation.7 | convolution fusion | flops 1073741824 | bytes 3145728 | tf_op jit(solution)/shard_map/dot_general | solution.py:41
  103.0 4.5 %gather_fusion = f32[512]{0:T(512)S(1)} fusion(f32[512,512]{1,0:T(8,128)S(1)} %fusion.2, s32[512]{0:T(512)S(1)} %bitcast.54), kind=kCustom, calls=%fused_computation | custom fusion | bytes 8192 | tf_op jit(solution)/shard_map/jit(diagonal)/cond/branch_0_fun/gather | solution.py:73
  107.5 0.1 subtract_add_fusion
  107.6 5.2 %convolution_bitcast_fusion = f32[1024,512]{0,1:T(8,128)S(1)} fusion(bf16[512,2048]{0,1:T(8,128)(2,1)} %bitcast.8, bf16[1024,2048]{1,0:T(8,128)(2,1)} %bitcast.63), kind=kOutput, calls=%fused_computation.6 | convolution fusion | flops 2147483648 | bytes 8388608 | tf_op jit(solution)/shard_map/dot_general | solution.py:38
  112.8 0.0 copy-start.1
  112.8 2.1 fusion.34
  114.9 2.2 fusion.30
  117.1 2.1 fusion.26
  119.3 0.0 copy-done.1
  119.3 1.5 fusion.22
  120.8 0.2 multiply_reduce_fusion.1
  121.0 0.3 fusion.58
  121.2 11.8 %psum.70 = f32[32,128]{1,0:T(8,128)S(1)} all-reduce(f32[32,128]{1,0:T(8,128)S(1)} %fusion.58), channel_id=1, replica_groups=mesh['py_0'=4,'py_1'=2,'px_0'=2,'px_1'=8,'px_2'=2] {'py_0'}, use_global_device_ids=true, to_apply=%region_5.6 | all-reduce | flops 4096 | bytes 32768 | tf_op jit(solution)/shard_map/psum | solution.py:34
  133.0 6.4 %psum.71 = f32[32,128]{1,0:T(8,128)S(1)} all-reduce(f32[32,128]{1,0:T(8,128)S(1)} %psum.70), channel_id=1, replica_groups=mesh['py_0'=4,'py_1'=2,'px_0'=2,'px_1'=8,'px_2'=2] {'py_1'}, use_global_device_ids=true, to_apply=%region_6.7 | all-reduce | flops 4096 | bytes 32768 | tf_op jit(solution)/shard_map/psum | solution.py:34
  139.4 7.5 %psum.72 = f32[32,128]{1,0:T(8,128)S(1)} all-reduce(f32[32,128]{1,0:T(8,128)S(1)} %psum.71), channel_id=1, replica_groups=mesh['py_0'=4,'py_1'=2,'px_0'=2,'px_1'=8,'px_2'=2] {'px_0'}, use_global_device_ids=true, to_apply=%region_7.8 | all-reduce | flops 4096 | bytes 32768 | tf_op jit(solution)/shard_map/psum | solution.py:34
  146.9 22.3 %psum.73 = f32[32,128]{1,0:T(8,128)S(1)} all-reduce(f32[32,128]{1,0:T(8,128)S(1)} %psum.72), channel_id=1, replica_groups=mesh['py_0'=4,'py_1'=2,'px_0'=2,'px_1'=8,'px_2'=2] {'px_1'}, use_global_device_ids=true, to_apply=%region_8.9 | all-reduce | flops 4096 | bytes 32768 | tf_op jit(solution)/shard_map/psum | solution.py:34
  169.3 18.9 %psum.74 = f32[32,128]{1,0:T(8,128)S(1)} all-reduce(f32[32,128]{1,0:T(8,128)S(1)} %psum.73), channel_id=1, replica_groups=mesh['py_0'=4,'py_1'=2,'px_0'=2,'px_1'=8,'px_2'=2] {'px_2'}, use_global_device_ids=true, to_apply=%region_9.10 | all-reduce | flops 4096 | bytes 32768 | tf_op jit(solution)/shard_map/psum | solution.py:34
  188.2 0.2 convolution_bitcast_fusion.2
  188.3 0.0 copy-start.2
  188.3 0.2 broadcast_multiply_fusion.1
  188.6 1.4 copy-done.2
  189.9 2.1 fusion.19
  192.1 2.1 fusion.15
  194.2 2.0 fusion.11
  196.3 1.4 fusion.7
  197.8 0.0 copy-start
  197.8 1.3 copy-done
  199.1 0.2 multiply_reduce_fusion
  199.3 0.3 fusion.56
  199.6 11.1 %psum.75 = f32[32,128]{1,0:T(8,128)S(1)} all-reduce(f32[32,128]{1,0:T(8,128)S(1)} %fusion.56), channel_id=1, replica_groups=mesh['py_0'=4,'py_1'=2,'px_0'=2,'px_1'=8,'px_2'=2] {'py_0'}, use_global_device_ids=true, to_apply=%region_11.12 | all-reduce | flops 4096 | bytes 32768 | tf_op jit(solution)/shard_map/psum | solution.py:34
  210.7 5.0 %psum.76 = f32[32,128]{1,0:T(8,128)S(1)} all-reduce(f32[32,128]{1,0:T(8,128)S(1)} %psum.75), channel_id=1, replica_groups=mesh['py_0'=4,'py_1'=2,'px_0'=2,'px_1'=8,'px_2'=2] {'py_1'}, use_global_device_ids=true, to_apply=%region_12.13 | all-reduce | flops 4096 | bytes 32768 | tf_op jit(solution)/shard_map/psum | solution.py:34
  215.7 9.4 %psum.77 = f32[32,128]{1,0:T(8,128)S(1)} all-reduce(f32[32,128]{1,0:T(8,128)S(1)} %psum.76), channel_id=1, replica_groups=mesh['py_0'=4,'py_1'=2,'px_0'=2,'px_1'=8,'px_2'=2] {'px_0'}, use_global_device_ids=true, to_apply=%region_13.14 | all-reduce | flops 4096 | bytes 32768 | tf_op jit(solution)/shard_map/psum | solution.py:34
  225.1 20.1 %psum.78 = f32[32,128]{1,0:T(8,128)S(1)} all-reduce(f32[32,128]{1,0:T(8,128)S(1)} %psum.77), channel_id=1, replica_groups=mesh['py_0'=4,'py_1'=2,'px_0'=2,'px_1'=8,'px_2'=2] {'px_1'}, use_global_device_ids=true, to_apply=%region_14.15 | all-reduce | flops 4096 | bytes 32768 | tf_op jit(solution)/shard_map/psum | solution.py:34
  245.2 17.6 %psum.79 = f32[32,128]{1,0:T(8,128)S(1)} all-reduce(f32[32,128]{1,0:T(8,128)S(1)} %psum.78), channel_id=1, replica_groups=mesh['py_0'=4,'py_1'=2,'px_0'=2,'px_1'=8,'px_2'=2] {'px_2'}, use_global_device_ids=true, to_apply=%region_15.16 | all-reduce | flops 4096 | bytes 32768 | tf_op jit(solution)/shard_map/psum | solution.py:34
  262.8 0.2 convolution_bitcast_fusion.1
  263.0 1.8 broadcast_multiply_fusion
  264.8 1.8 copy.51
  (10 shorter events, 0.3 us)
Async XLA Ops:
  24.2 12.8 %all-to-all-start.1 = ((bf16[8,512,64]{1,2,0:T(8,128)(2,1)}), bf16[8,512,64]{1,2,0:T(8,128)(2,1)S(1)}, u32[]{:S(2)}, u32[]{:S(2)}) async-start(bf16[8,512,64]{1,2,0:T(8,128)(2,1)} %broadcast_in_dim.12), calls=%async_computation.1 | async-start | bytes 1048576 | tf_op jit(solution)/shard_map/all_to_all | solution.py:26
  42.3 6.2 %copy-start.3 = (f32[64,16,512]{2,1,0:T(8,128)S(1)}, f32[64,16,512]{2,1,0:T(8,128)}, u32[]{:S(2)}) copy-start(f32[64,16,512]{2,1,0:T(8,128)} %param.22) | copy-start | bytes 6291460
  42.3 57.1 %all-to-all-start.2 = ((bf16[32,512,64]{1,2,0:T(8,128)(2,1)}), bf16[32,512,64]{1,2,0:T(8,128)(2,1)}, u32[]{:S(2)}, u32[]{:S(2)}) async-start(bf16[32,512,64]{1,2,0:T(8,128)(2,1)} %reshape.225), calls=%async_computation.2 | async-start | bytes 4194304 | tf_op jit(solution)/shard_map/all_to_all | solution.py:69
  48.6 3.2 %copy-start.4 = (s32[1,1,4]{2,1,0:T(1,128)S(1)}, s32[1,1,4]{2,1,0:T(1,128)}, u32[]{:S(2)}) copy-start(s32[1,1,4]{2,1,0:T(1,128)} %param.23) | copy-start | bytes 52
  112.8 6.5 %copy-start.1 = (f32[1024,512]{0,1:T(8,128)}, f32[1024,512]{0,1:T(8,128)S(1)}, u32[]{:S(2)}) copy-start(f32[1024,512]{0,1:T(8,128)S(1)} %convolution_bitcast_fusion) | copy-start | bytes 6291460
  188.3 1.6 copy-start.2
  197.8 1.3 copy-start
where the time goes:
time: 267 us
  blocking collectives  152 us (57%)
  waiting for transfers between devices  54.2 us (20%)
  matrix products  25.8 us (10%)
  local copies, waits for them, and re-layouts  18.1 us (7%)
  starting transfers between devices  10.4 us (4%)
  other arithmetic  5.86 us (2%)
    psum x10, blocking collectives, over_axes(): return functools.reduce(lax.psum, axes, value)  130 us
    all_to_all x1, waiting for transfers between devices, per_device(): lax.all_to_all(outgoing, PX, split_axis=0, concat_axis=2, tiled=True)  45.6 us
    all_to_all x1, blocking collectives, sent_to_all(): return lax.all_to_all(copies, axis, split_axis=0, concat_axis=0, tiled=True)  21.9 us
    dot_general x8, matrix products, per_device(): jnp.dot(current, gram[:, low:low + BLK], precision=lax.Precision.HIGHEST)  15.4 us
    all_to_all x1, waiting for transfers between devices, sent_to_all(): return lax.all_to_all(copies, axis, split_axis=0, concat_axis=0, tiled=True)  8.61 us
    all_to_all x1, starting transfers between devices, per_device(): lax.all_to_all(outgoing, PX, split_axis=0, concat_axis=2, tiled=True)  6.22 us
  transfers between devices with their start and end apart: 2, of which 2 were waited for; matrix products, arithmetic and copies ran while one was open for 2% of the time, Pallas kernels for 0%

commit v1 on v0

v1 whole, which is shorter than its diff:
```python
import jax
import jax.numpy as jnp
from jax import lax
from jax.experimental import pallas as pl
from jax.experimental.pallas import tpu as pltpu
from jax.sharding import Mesh
from jax.sharding import PartitionSpec as P

BLK = 128
SLOTS = 4
WIDTH = SLOTS * BLK
NBLK = 32
ITERS = 2
PY = ("py_0", "py_1")
PX = ("px_0", "px_1", "px_2")
EVERY = ("py_0", "py_1", "px_0", "px_1", "px_2")
COLUMN = ("py_0", "py_1", "px_1")
PLANE = ("py_0", "py_1", "px_0", "px_2")
CORE_MATES = ("py_0", "py_1", "px_0", "px_1")
CORE = "px_2"


def to_everyone(value, axes):
    copies = jnp.broadcast_to(value[None], (lax.axis_size(axes), *value.shape))
    return lax.all_to_all(copies, axes, split_axis=0, concat_axis=0, tiled=True)


def select_kernel(place_ref, ids_ref, rows_ref, out_ref):
    tiles = out_ref.shape[0]

    @pl.loop(0, tiles)
    def _(tile):
        for slot in range(SLOTS):
            block = ids_ref[tile ^ place_ref[0, 0], slot]
            live = block < NBLK
            safe = jnp.where(live, block, 0)
            group = safe // SLOTS
            lane = pl.multiple_of((safe % SLOTS) * BLK, BLK)

            @pl.when(live)
            def _():
                out_ref[tile, :, :, slot * BLK : (slot + 1) * BLK] = rows_ref[
                    group, :, :, pl.ds(lane, BLK)
                ]

            @pl.when(jnp.logical_not(live))
            def _():
                out_ref[tile, :, :, slot * BLK : (slot + 1) * BLK] = jnp.zeros(
                    (rows_ref.shape[1], 8, BLK), out_ref.dtype
                )


def select(place, tile_ids, rows):
    tiles = tile_ids.shape[0]
    return pl.pallas_call(
        select_kernel,
        out_shape=jax.ShapeDtypeStruct((tiles, *rows.shape[1:]), rows.dtype),
        in_specs=[
            pl.BlockSpec(memory_space=pltpu.SMEM),
            pl.BlockSpec(memory_space=pltpu.SMEM),
            pl.BlockSpec(memory_space=pltpu.VMEM),
        ],
        out_specs=pl.BlockSpec(memory_space=pltpu.VMEM),
        cost_estimate=pl.CostEstimate(flops=1 << 20, bytes_accessed=1 << 22, transcendentals=0),
        name="select",
    )(place, tile_ids, rows)


def totals_of(colsq, mate_ids, my_ids, peer_ids):
    seen = to_everyone(colsq, CORE_MATES).reshape(-1, BLK)
    wanted = jnp.concatenate([my_ids, peer_ids])
    match = (wanted[:, None] == mate_ids.reshape(1, -1)).astype(jnp.float32)
    sums = jnp.dot(match, seen, precision=lax.Precision.HIGHEST)
    other = lax.ppermute(sums[SLOTS:], CORE, [(0, 1), (1, 0)])
    return sums[:SLOTS] + other


def swapped(value, axis, bit):
    size = lax.axis_size(axis)
    return lax.ppermute(value, axis, [(i, i ^ bit) for i in range(size)])


def doubled(ids, axis):
    bit = 1
    while bit < lax.axis_size(axis):
        ids = jnp.concatenate([ids, swapped(ids, axis, bit)])
        bit *= 2
    return ids


def in_place_order(value, dim, axis):
    size = value.shape[dim]
    at = lax.axis_index(axis)
    bit = 1
    while bit < size:
        shape = (*value.shape[:dim], size // (2 * bit), 2, bit, *value.shape[dim + 1 :])
        flipped = jnp.flip(value.reshape(shape), dim + 1).reshape(value.shape)
        value = jnp.where((at & bit) != 0, flipped, value)
        bit *= 2
    return value


def per_device(movie, traces, footprints, block_ids):
    rows, cols, frames = movie.shape
    pixels = rows * cols
    n_group = lax.axis_size(PY)
    n_z = lax.axis_size("px_1")
    sizes = tuple(lax.axis_size(a) for a in EVERY)
    part = traces.shape[1] // n_group
    my_ids = block_ids.reshape(SLOTS)
    pieces = traces.T.reshape(n_group, 1, part, traces.shape[0])
    pieces = jnp.broadcast_to(pieces, (n_group, n_z, part, traces.shape[0]))
    pieces = pieces.reshape(n_group * n_z, part, traces.shape[0])
    spread = lax.all_to_all(pieces, COLUMN, split_axis=0, concat_axis=0, tiled=True)
    plane_ids = my_ids[None]
    for axis in reversed(PLANE):
        plane_ids = doubled(plane_ids, axis)
    every_ids = doubled(plane_ids, "px_1")
    peer_ids = plane_ids[1]
    mate_ids = every_ids.reshape(n_z, *sizes[:3], sizes[4], SLOTS)[:, :, :, :, 0]
    mate_ids = mate_ids.transpose(1, 2, 3, 0, 4)
    for dim, axis in enumerate(CORE_MATES):
        mate_ids = in_place_order(mate_ids, dim, axis)
    place = lax.axis_index(PLANE).reshape(1, 1)

    outgoing = select(place, plane_ids, spread.reshape(n_group, n_z, part, traces.shape[0]))
    received = lax.all_to_all(outgoing, PLANE, split_axis=0, concat_axis=0, tiled=True)
    picked = received.reshape(n_group, sizes[2], sizes[4], n_z, part, WIDTH)
    picked = picked.transpose(1, 3, 2, 0, 4, 5).reshape(frames, WIDTH)

    tile_movie = movie.reshape(pixels, frames)
    cross = lax.dot_general(
        tile_movie, picked, (((1,), (0,)), ((), ())), preferred_element_type=jnp.float32
    )
    gram = lax.dot_general(
        picked, picked, (((0,), (0,)), ((), ())), preferred_element_type=jnp.float32
    )
    live = (my_ids < NBLK).astype(jnp.float32)
    column_live = jnp.repeat(live, BLK)
    wide = picked.astype(jnp.float32)
    denom = jnp.sum(wide * wide, axis=0) + 1e-06 + (1.0 - column_live)
    current = footprints.reshape(pixels, WIDTH) * column_live[None, :]
    pixall = pixels * lax.axis_size(EVERY)
    for step in range(ITERS):
        for slot in range(SLOTS):
            low = slot * BLK
            resid = cross[:, low : low + BLK] - jnp.dot(
                current, gram[:, low : low + BLK], precision=lax.Precision.HIGHEST
            )
            fresh = jnp.maximum(
                current[:, low : low + BLK] + resid / denom[None, low : low + BLK], 0.0
            )
            current = current.at[:, low : low + BLK].set(fresh)
        colsq = jnp.sum(current * current, axis=0).reshape(SLOTS, BLK)
        totals = totals_of(colsq, mate_ids, my_ids, peer_ids)
        scale = live[:, None] / jnp.sqrt(totals / pixall + 1e-06)
        current = current * scale.reshape(1, WIDTH)
    return current.reshape(rows, cols, WIDTH)


def solution(mesh):
    finer = Mesh(mesh.devices.reshape(4, 2, 2, 8, 2), EVERY)
    placed = (P(PY, PX, None), P(PY, PX), P(PY, PX, None), P(PY, PX, None))
    return jax.shard_map(
        per_device, mesh=finer, in_specs=placed, out_specs=P(PY, PX, None), check_vma=False
    )
```

time: 267 us -> 165 us (0.62)
  blocking collectives: 152 us -> 20 us
  starting transfers between devices: 10.4 us -> 58 us
  waiting for transfers between devices: 54.2 us -> 30.8 us
  Pallas kernels: 0 us -> 5.62 us
  other arithmetic: 5.86 us -> 10.8 us
  matrix products: 25.8 us -> 21.8 us
    psum x10 -> x0, blocking collectives: 130 us -> none  [over_axes(): return functools.reduce(lax.psum, axes, value)]
    all_to_all x2 -> x3, waiting for transfers between devices: 54.2 us -> 20.1 us  [the longest x1 11.1 us: to_everyone(): return lax.all_to_all(copies, axes, split_axis=0, concat_axis=0, tiled=True)]
    all_to_all x2 -> x3, starting transfers between devices: 10.4 us -> 36.1 us  [the longest x1 13.5 us: per_device(): lax.all_to_all(pieces, COLUMN, split_axis=0, concat_axis=0, tiled=True)]
    ppermute x0 -> x10, starting transfers between devices: none -> 22 us  [the longest x8 18 us: swapped(): return lax.ppermute(value, axis, [(i, i ^ bit) for i in range(size)])]
    ppermute x0 -> x10, waiting for transfers between devices: none -> 10.7 us  [the longest x8 9.08 us: swapped(): return lax.ppermute(value, axis, [(i, i ^ bit) for i in range(size)])]
    pallas_call x0 -> x1, Pallas kernels: none -> 5.62 us  [select(): pl.pallas_call(select_kernel, out_shape=jax.ShapeDtypeStruct((tiles, *row...]
    gather x1 -> x0, local copies, waits for them, and re-layouts: 4.52 us -> none  [per_device(): denom = jnp.diagonal(gram) + 1e-06 + (1.0 - column_live)]
    concatenate x0 -> x6, local copies, waits for them, and re-layouts: none -> 3.54 us  [doubled(): ids = jnp.concatenate([ids, swapped(ids, axis, bit)])]
  transfers between devices with their start and end apart: 2 -> 13, of which waited for: 2 -> 12; matrix products, arithmetic and copies ran while one was open for 2% -> 9% of each run, Pallas kernels for 0% -> 0%
where the time goes in v1:
time: 165 us
  starting transfers between devices  58 us (35%)
  waiting for transfers between devices  30.8 us (19%)
  matrix products  21.8 us (13%)
  blocking collectives  20 us (12%)
  local copies, waits for them, and re-layouts  17.2 us (10%)
  other arithmetic  10.8 us (7%)
  Pallas kernels  5.62 us (3%)
    all_to_all x1, blocking collectives, to_everyone(): return lax.all_to_all(copies, axes, split_axis=0, concat_axis=0, tiled=True)  20 us
    ppermute x8, starting transfers between devices, swapped(): return lax.ppermute(value, axis, [(i, i ^ bit) for i in range(size)])  18 us
    dot_general x8, matrix products, per_device(): jnp.dot(current, gram[:, low:low + BLK], precision=lax.Precision.HIGHEST)  14.9 us
    all_to_all x1, starting transfers between devices, per_device(): lax.all_to_all(pieces, COLUMN, split_axis=0, concat_axis=0, tiled=True)  13.5 us
    all_to_all x1, starting transfers between devices, to_everyone(): return lax.all_to_all(copies, axes, split_axis=0, concat_axis=0, tiled=True)  11.7 us
    all_to_all x1, waiting for transfers between devices, to_everyone(): return lax.all_to_all(copies, axes, split_axis=0, concat_axis=0, tiled=True)  11.1 us
    all_to_all x1, starting transfers between devices, per_device(): lax.all_to_all(outgoing, PLANE, split_axis=0, concat_axis=0, tiled=True)  10.9 us
    ppermute x8, waiting for transfers between devices, swapped(): return lax.ppermute(value, axis, [(i, i ^ bit) for i in range(size)])  9.08 us
  transfers between devices with their start and end apart: 13, of which 12 were waited for; matrix products, arithmetic and copies ran while one was open for 9% of the time, Pallas kernels for 0%

profile of v1, /device:TPU:1, one launch (start us, length us, event | category | flops | bytes accessed | tf_op | source)
XLA Modules:
  0.0 164.7 jit_solution(14719490412950837342)
XLA Ops:
  0.0 1.7 %broadcast_in_dim.16 = bf16[8,8,8,512]{3,2,1,0:T(8,128)(2,1)} broadcast(bf16[8,8,512]{2,1,0:T(8,128)(2,1)} %bitcast.85), dimensions={0,2,3} | broadcast | bytes 589824 | tf_op jit(solution)/shard_map/broadcast_in_dim | solution.py:112
  1.7 13.5 %all-to-all-start = ((bf16[64,8,512]{2,1,0:T(8,128)(2,1)}), bf16[64,8,512]{2,1,0:T(8,128)(2,1)S(1)}, u32[]{:S(2)}, u32[]{:S(2)}) async-start(bf16[64,8,512]{2,1,0:T(8,128)(2,1)} %bitcast.7), calls=%async_computation | async-start | bytes 1048576 | tf_op jit(solution)/shard_map/all_to_all | solution.py:114
  15.2 1.0 collective-permute-start
  16.2 1.0 collective-permute-done
  17.2 0.7 pad_add_fusion.2
  17.8 2.6 %collective-permute-start.1 = (s32[2,4]{1,0:T(2,128)S(1)}, s32[2,4]{1,0:T(2,128)S(1)}, u32[]{:S(2)}, u32[]{:S(2)}) collective-permute-start(s32[2,4]{1,0:T(2,128)S(1)} %pad_add_fusion.2), channel_id=1, source_target_pairs={{0,16},{16,0},{1,17},{17,1},{2,18},{18,2},{3,19},{19,3},{4,20},{20... | collective-permute-start | bytes 104 | tf_op jit(solution)/shard_map/ppermute | solution.py:80
  20.4 1.6 collective-permute-done.1
  22.0 0.7 pad_add_fusion.1
  22.7 1.3 collective-permute-start.2
  24.0 1.4 collective-permute-done.2
  25.4 0.7 pad_add_fusion
  26.1 1.3 collective-permute-start.3
  27.4 1.5 collective-permute-done.3
  28.9 0.7 concatenate.54
  29.6 2.9 %collective-permute-start.4 = (s32[16,4]{1,0:T(8,128)S(1)}, s32[16,4]{1,0:T(8,128)S(1)}, u32[]{:S(2)}, u32[]{:S(2)}) collective-permute-start(s32[16,4]{1,0:T(8,128)S(1)} %concatenate.54), channel_id=1, source_target_pairs={{0,128},{64,192},{128,0},{192,64},{1,129},{65,193},{129,1},{193,65... | collective-permute-start | bytes 776 | tf_op jit(solution)/shard_map/ppermute | solution.py:80
  32.5 1.5 collective-permute-done.4
  34.0 2.4 %concatenate.55.ids_ref = s32[32,4]{1,0:T(8,128)} concatenate(s32[1,4]{1,0:T(1,128)} %bitcast.91, s32[1,4]{1,0:T(1,128)S(1)} %collective-permute-done, s32[2,4]{1,0:T(2,128)S(1)} %collective-permute-done.1, s32[4,4]{1,0:T(4,128)S(1)} %collective-permute-done.2, s32[8,4]{1,0:T(8,128)S(1)} %collective-permute-done.3, s32[16,4]{1,0:T(8,128)S(1)} %collective-permute-done.4), dimensions={0} | concatenate | bytes 1024 | tf_op jit(solution)/shard_map/concatenate | solution.py:86
  36.4 0.8 copy-done.3
  37.2 5.6 %select.41 = bf16[32,8,8,512]{3,2,1,0:T(8,128)(2,1)} custom-call(s32[1,1]{1,0:T(1,128)} %bitcast.3.place_ref, s32[32,4]{1,0:T(8,128)} %concatenate.55.ids_ref, bf16[8,8,8,512]{3,2,1,0:T(8,128)(2,1)} %bitcast.73), custom_call_target="tpu_custom_call" | custom-call | flops 1048576 | bytes 4194304 | tf_op jit(solution)/shard_map/select/pallas_call | solution.py:55
  42.9 10.9 %all-to-all-start.1 = ((bf16[32,8,8,512]{3,2,1,0:T(8,128)(2,1)}), bf16[32,8,8,512]{3,2,1,0:T(8,128)(2,1)}, u32[]{:S(2)}, u32[]{:S(2)}) async-start(bf16[32,8,8,512]{3,2,1,0:T(8,128)(2,1)} %select.41), calls=%async_computation.1 | async-start | bytes 4194304 | tf_op jit(solution)/shard_map/all_to_all | solution.py:127
  53.8 1.8 %copy.145 = f32[1024,512]{0,1:T(8,128)} copy(f32[1024,512]{1,0:T(8,128)S(1)} %bitcast.71) | data formatting | bytes 4194304 | tf_op jit(solution)/shard_map/reshape | solution.py:142
  55.7 1.8 %broadcast_multiply_fusion.2 = f32[1024,512]{0,1:T(8,128)S(1)} fusion(f32[1024,512]{0,1:T(8,128)} %copy.145, f32[512]{0:T(512)S(1)} %broadcast_bitcast_fusion), kind=kLoop, calls=%fused_computation.47 | loop fusion | flops 524288 | bytes 4196352 | tf_op jit(solution)/shard_map/mul | solution.py:142
  57.5 1.4 collective-permute-start.5
  59.4 1.2 collective-permute-done.5
  60.7 2.1 %collective-permute-start.6 = (s32[64,4]{0,1:T(4,128)S(1)}, s32[64,4]{0,1:T(4,128)S(1)}, u32[]{:S(2)}, u32[]{:S(2)}) collective-permute-start(s32[64,4]{0,1:T(4,128)S(1)} %concatenate.57), channel_id=1, source_target_pairs={{0,4},{2,6},{4,0},{6,2},{8,12},{10,14},{12,8},{14,10},{1,5},{3,7},... | collective-permute-start | bytes 3080 | tf_op jit(solution)/shard_map/ppermute | solution.py:80
  62.8 0.6 compare_reduce_fusion.2
  63.4 0.7 compare_reduce_fusion
  64.2 0.3 collective-permute-done.6
  64.6 5.4 %collective-permute-start.7 = (s32[128,4]{0,1:T(4,128)S(1)}, s32[128,4]{0,1:T(4,128)S(1)}, u32[]{:S(2)}, u32[]{:S(2)}) collective-permute-start(s32[128,4]{0,1:T(4,128)S(1)} %concatenate.58), channel_id=1, source_target_pairs={{0,8},{2,10},{4,12},{6,14},{8,0},{10,2},{12,4},{14,6},{1,9},{3,11}... | collective-permute-start | bytes 6152 | tf_op jit(solution)/shard_map/ppermute | solution.py:80
  70.0 0.6 pad_add_fusion.3
  70.6 0.6 collective-permute-done.7
  71.8 0.6 rev.26
  72.5 8.9 %all-to-all-done.1 = bf16[32,8,8,512]{3,2,1,0:T(8,128)(2,1)} async-done(((bf16[32,8,8,512]{3,2,1,0:T(8,128)(2,1)}), bf16[32,8,8,512]{3,2,1,0:T(8,128)(2,1)}, u32[]{:S(2)}, u32[]{:S(2)}) %all-to-all-start.1) | async-done | bytes 2097184 | tf_op jit(solution)/shard_map/all_to_all | solution.py:127
  81.4 2.1 %multiply_reduce_fusion = f32[512]{0:T(512)S(1)} fusion(bf16[8,2,2,8,8,512]{5,4,3,2,1,0:T(8,128)(2,1)} %bitcast.9), kind=kLoop, calls=%fused_computation | loop fusion | flops 3145216 | bytes 2099200 | tf_op jit(solution)/shard_map/reduce_sum | solution.py:141
  83.5 3.5 %fusion.2 = f32[512,512]{1,0:T(8,128)S(1)} fusion(bf16[8,2,2,8,8,512]{5,4,3,2,1,0:T(8,128)(2,1)} %bitcast.9), kind=kOutput, calls=%fused_computation.6 | convolution fusion | flops 1073741824 | bytes 3145728 | tf_op jit(solution)/shard_map/dot_general | solution.py:135
  87.0 2.0 %copy.146 = bf16[8,2,2,8,8,512]{5,4,0,2,3,1:T(8,128)(2,1)S(1)} copy(bf16[8,2,2,8,8,512]{5,4,3,2,1,0:T(8,128)(2,1)} %bitcast.9) | data formatting | bytes 4194304 | tf_op jit(solution)/shard_map/reshape | solution.py:128
  89.1 0.7 copy-done.9
  89.8 2.4 %convolution_bitcast_fusion = f32[1024,512]{0,1:T(8,128)S(1)} fusion(bf16[2048,512]{1,0:T(8,128)(2,1)S(1)} %bitcast.72, bf16[1024,2048]{1,0:T(8,128)(2,1)S(1)} %bitcast.97), kind=kOutput, calls=%fused_computation.5 | convolution fusion | flops 2147483648 | bytes 8388608 | tf_op jit(solution)/shard_map/dot_general | solution.py:132
  92.2 2.0 %fusion.34 = f32[1024,128]{0,1:T(8,128)S(1)} fusion(f32[1024,512]{0,1:T(8,128)S(1)} %broadcast_multiply_fusion.2, f32[1024,512]{0,1:T(8,128)S(1)} %convolution_bitcast_fusion, f32[128]{0:T(128)S(1)} %get-tuple-element.104, pred[]{:T(512)} %compare_reduce_fusion.2, f32[512,512]{1,0:T(8,128)S(1)} %fusion.2), kind=kOutput, calls=%fused_computation.44 | convolution fusion | flops 805961728 | bytes 3932673 | tf_op jit(solution)/shard_map/dot_general | solution.py:147
  94.3 2.1 %fusion.30 = f32[1024,128]{0,1:T(8,128)S(1)} fusion(f32[1024,512]{0,1:T(8,128)S(1)} %constant_dynamic-update-slice_fusion.7, f32[1024,512]{0,1:T(8,128)S(1)} %convolution_bitcast_fusion, f32[128]{0:T(128)S(1)} %get-tuple-element.103, pred[]{:T(512)} %get-tuple-element.106, f32[512,512]{1,0:T(8,128)S(1)} %fusion.2), kind=kOutput, calls=%fused_computation.39 | convolution fusion | flops 805961728 | bytes 3932673 | tf_op jit(solution)/shard_map/dot_general | solution.py:147
  96.4 2.0 %fusion.26 = f32[1024,128]{0,1:T(8,128)S(1)} fusion(f32[1024,512]{0,1:T(8,128)S(1)} %constant_dynamic-update-slice_fusion.6, f32[1024,512]{0,1:T(8,128)S(1)} %convolution_bitcast_fusion, f32[128]{0:T(128)S(1)} %get-tuple-element.102, pred[]{:T(512)} %get-tuple-element.105, f32[512,512]{1,0:T(8,128)S(1)} %fusion.2), kind=kOutput, calls=%fused_computation.34 | convolution fusion | flops 805961728 | bytes 3932673 | tf_op jit(solution)/shard_map/dot_general | solution.py:147
  98.5 1.4 fusion.22
  99.9 0.2 multiply_reduce_fusion.2
  100.1 0.8 broadcast_in_dim.18
  100.9 11.7 %all-to-all-start.2 = ((f32[128,4,128]{2,1,0:T(4,128)}), f32[128,4,128]{2,1,0:T(4,128)S(1)}, u32[]{:S(2)}, u32[]{:S(2)}) async-start(f32[128,4,128]{2,1,0:T(4,128)} %broadcast_in_dim.18), calls=%async_computation.2 | async-start | bytes 524288 | tf_op jit(solution)/shard_map/all_to_all | solution.py:25
  112.6 0.9 bitcast_select_fusion.2
  113.5 0.6 rev.27
  114.1 0.9 bitcast_select_fusion.1
  115.2 11.1 %all-to-all-done.2 = f32[128,4,128]{2,1,0:T(4,128)S(1)} async-done(((f32[128,4,128]{2,1,0:T(4,128)}), f32[128,4,128]{2,1,0:T(4,128)S(1)}, u32[]{:S(2)}, u32[]{:S(2)}) %all-to-all-start.2) | async-done | bytes 262176 | tf_op jit(solution)/shard_map/all_to_all | solution.py:25
  126.4 0.9 fusion.45
  127.2 2.4 %collective-permute-start.8 = (f32[4,128]{1,0:T(4,128)S(1)}, f32[4,128]{1,0:T(4,128)S(1)}, u32[]{:S(2)}, u32[]{:S(2)}) collective-permute-start(f32[4,128]{1,0:T(4,128)S(1)} %slice.241), channel_id=1, source_target_pairs={{0,1},{1,0},{2,3},{3,2},{4,5},{5,4},{6,7},{7,6},{8,9},{9,8},{10,11... | collective-permute-start | bytes 6152 | tf_op jit(solution)/shard_map/ppermute | solution.py:74
  129.6 0.8 collective-permute-done.8
  130.7 1.4 copy-done.1
  132.1 2.0 %fusion.19 = f32[1024,128]{0,1:T(8,128)S(1)} fusion(f32[1024,512]{0,1:T(8,128)S(1)} %broadcast_multiply_fusion.1, f32[1024,512]{0,1:T(8,128)S(1)} %copy-done.1, f32[128]{0:T(128)S(1)} %copy-done.7, pred[]{:T(512)} %compare_reduce_fusion.2, f32[512,512]{1,0:T(8,128)S(1)} %fusion.2), kind=kOutput, calls=%fused_computation.25 | convolution fusion | flops 805961728 | bytes 3932673 | tf_op jit(solution)/shard_map/dot_general | solution.py:147
  134.1 2.1 %fusion.15 = f32[1024,128]{0,1:T(8,128)S(1)} fusion(f32[1024,512]{0,1:T(8,128)S(1)} %constant_dynamic-update-slice_fusion.3, f32[1024,512]{0,1:T(8,128)S(1)} %copy-done.1, f32[128]{0:T(128)S(1)} %get-tuple-element.103, pred[]{:T(512)} %get-tuple-element.106, f32[512,512]{1,0:T(8,128)S(1)} %fusion.2), kind=kOutput, calls=%fused_computation.20 | convolution fusion | flops 805961728 | bytes 3932673 | tf_op jit(solution)/shard_map/dot_general | solution.py:147
  136.2 2.0 %fusion.11 = f32[1024,128]{0,1:T(8,128)S(1)} fusion(f32[1024,512]{0,1:T(8,128)S(1)} %constant_dynamic-update-slice_fusion.2, f32[1024,512]{0,1:T(8,128)S(1)} %copy-done.1, f32[128]{0:T(128)S(1)} %get-tuple-element.102, pred[]{:T(512)} %get-tuple-element.105, f32[512,512]{1,0:T(8,128)S(1)} %fusion.2), kind=kOutput, calls=%fused_computation.15 | convolution fusion | flops 805961728 | bytes 3932673 | tf_op jit(solution)/shard_map/dot_general | solution.py:147
  138.3 1.4 fusion.7
  139.7 0.2 multiply_reduce_fusion.1
  140.0 20.0 %all_to_all.20 = f32[128,4,128]{2,1,0:T(4,128)S(1)} all-to-all(f32[128,4,128]{2,1,0:T(4,128)S(1)} %broadcast_in_dim.20), channel_id=1, replica_groups=mesh['py_0'=4,'py_1'=2,'px_0'=2,'px_1'=8,'px_2'=2] {'py_0','py_1','px_0'..., dimensions={0} | all-to-all | bytes 524288 | tf_op jit(solution)/shard_map/all_to_all | solution.py:25
  160.0 0.2 fusion.43
  160.2 1.6 collective-permute-start.9
  161.8 0.8 collective-permute-done.9
  162.7 0.2 broadcast_multiply_fusion
  162.9 1.8 %copy.178 = f32[1024,512]{1,0:T(8,128)} copy(f32[1024,512]{0,1:T(8,128)S(1)} %broadcast_multiply_fusion) | data formatting | bytes 4194304 | tf_op jit(solution)/shard_map/mul | solution.py:157
  (59 shorter events, 2.5 us)
Async XLA Ops:
  1.7 34.8 %all-to-all-start = ((bf16[64,8,512]{2,1,0:T(8,128)(2,1)}), bf16[64,8,512]{2,1,0:T(8,128)(2,1)S(1)}, u32[]{:S(2)}, u32[]{:S(2)}) async-start(bf16[64,8,512]{2,1,0:T(8,128)(2,1)} %bitcast.7), calls=%async_computation | async-start | bytes 1048576 | tf_op jit(solution)/shard_map/all_to_all | solution.py:114
  15.2 2.0 %collective-permute-start = (s32[1,4]{1,0:T(1,128)}, s32[1,4]{1,0:T(1,128)S(1)}, u32[]{:S(2)}, u32[]{:S(2)}) collective-permute-start(s32[1,4]{1,0:T(1,128)} %bitcast.86), channel_id=1, source_target_pairs={{0,1},{1,0},{2,3},{3,2},{4,5},{5,4},{6,7},{7,6},{8,9},{9,8},{10,11... | collective-permute-start | bytes 56 | tf_op jit(solution)/shard_map/ppermute | solution.py:80
  17.8 4.2 %collective-permute-start.1 = (s32[2,4]{1,0:T(2,128)S(1)}, s32[2,4]{1,0:T(2,128)S(1)}, u32[]{:S(2)}, u32[]{:S(2)}) collective-permute-start(s32[2,4]{1,0:T(2,128)S(1)} %pad_add_fusion.2), channel_id=1, source_target_pairs={{0,16},{16,0},{1,17},{17,1},{2,18},{18,2},{3,19},{19,3},{4,20},{20... | collective-permute-start | bytes 104 | tf_op jit(solution)/shard_map/ppermute | solution.py:80
  22.7 2.7 %collective-permute-start.2 = (s32[4,4]{1,0:T(4,128)S(1)}, s32[4,4]{1,0:T(4,128)S(1)}, u32[]{:S(2)}, u32[]{:S(2)}) collective-permute-start(s32[4,4]{1,0:T(4,128)S(1)} %pad_add_fusion.1), channel_id=1, source_target_pairs={{0,32},{32,0},{1,33},{33,1},{2,34},{34,2},{3,35},{35,3},{4,36},{36... | collective-permute-start | bytes 200 | tf_op jit(solution)/shard_map/ppermute | solution.py:80
  26.1 2.8 %collective-permute-start.3 = (s32[8,4]{1,0:T(8,128)S(1)}, s32[8,4]{1,0:T(8,128)S(1)}, u32[]{:S(2)}, u32[]{:S(2)}) collective-permute-start(s32[8,4]{1,0:T(8,128)S(1)} %pad_add_fusion), channel_id=1, source_target_pairs={{0,64},{64,0},{128,192},{192,128},{1,65},{65,1},{129,193},{193,129... | collective-permute-start | bytes 392 | tf_op jit(solution)/shard_map/ppermute | solution.py:80
  29.6 4.4 %collective-permute-start.4 = (s32[16,4]{1,0:T(8,128)S(1)}, s32[16,4]{1,0:T(8,128)S(1)}, u32[]{:S(2)}, u32[]{:S(2)}) collective-permute-start(s32[16,4]{1,0:T(8,128)S(1)} %concatenate.54), channel_id=1, source_target_pairs={{0,128},{64,192},{128,0},{192,64},{1,129},{65,193},{129,1},{193,65... | collective-permute-start | bytes 776 | tf_op jit(solution)/shard_map/ppermute | solution.py:80
  36.4 0.8 copy-start.3
  42.9 10.9 %copy-start.2 = (f32[64,16,512]{2,1,0:T(8,128)S(1)}, f32[64,16,512]{2,1,0:T(8,128)}, u32[]{:S(2)}) copy-start(f32[64,16,512]{2,1,0:T(8,128)} %param.22) | copy-start | bytes 6291460
  42.9 38.5 %all-to-all-start.1 = ((bf16[32,8,8,512]{3,2,1,0:T(8,128)(2,1)}), bf16[32,8,8,512]{3,2,1,0:T(8,128)(2,1)}, u32[]{:S(2)}, u32[]{:S(2)}) async-start(bf16[32,8,8,512]{3,2,1,0:T(8,128)(2,1)} %select.41), calls=%async_computation.1 | async-start | bytes 4194304 | tf_op jit(solution)/shard_map/all_to_all | solution.py:127
  53.8 1.8 %copy-start.5 = (s32[1,1,4]{2,1,0:T(1,128)S(1)}, s32[1,1,4]{2,1,0:T(1,128)}, u32[]{:S(2)}) copy-start(s32[1,1,4]{2,1,0:T(1,128)} %param.23) | copy-start | bytes 52
  55.7 1.8 %copy-start.4 = (s32[32,4]{1,0:T(8,128)S(1)}, s32[32,4]{1,0:T(8,128)}, u32[]{:S(2)}) copy-start(s32[32,4]{1,0:T(8,128)} %concatenate.55.ids_ref) | copy-start | bytes 1540
  57.5 3.1 %collective-permute-start.5 = (s32[32,4]{1,0:T(8,128)S(1)}, s32[32,4]{1,0:T(8,128)S(1)}, u32[]{:S(2)}, u32[]{:S(2)}) collective-permute-start(s32[32,4]{1,0:T(8,128)S(1)} %copy-done.4), channel_id=1, source_target_pairs={{0,2},{2,0},{4,6},{6,4},{8,10},{10,8},{12,14},{14,12},{1,3},{3,1},... | collective-permute-start | bytes 1544 | tf_op jit(solution)/shard_map/ppermute | solution.py:80
  60.7 3.8 %collective-permute-start.6 = (s32[64,4]{0,1:T(4,128)S(1)}, s32[64,4]{0,1:T(4,128)S(1)}, u32[]{:S(2)}, u32[]{:S(2)}) collective-permute-start(s32[64,4]{0,1:T(4,128)S(1)} %concatenate.57), channel_id=1, source_target_pairs={{0,4},{2,6},{4,0},{6,2},{8,12},{10,14},{12,8},{14,10},{1,5},{3,7},... | collective-permute-start | bytes 3080 | tf_op jit(solution)/shard_map/ppermute | solution.py:80
  64.6 6.6 %collective-permute-start.7 = (s32[128,4]{0,1:T(4,128)S(1)}, s32[128,4]{0,1:T(4,128)S(1)}, u32[]{:S(2)}, u32[]{:S(2)}) collective-permute-start(s32[128,4]{0,1:T(4,128)S(1)} %concatenate.58), channel_id=1, source_target_pairs={{0,8},{2,10},{4,12},{6,14},{8,0},{10,2},{12,4},{14,6},{1,9},{3,11}... | collective-permute-start | bytes 6152 | tf_op jit(solution)/shard_map/ppermute | solution.py:80
  87.0 2.8 %copy-start.9 = (bf16[64,16,2048]{2,1,0:T(8,128)(2,1)S(1)}, bf16[64,16,2048]{2,1,0:T(8,128)(2,1)}, u32[]{:S(2)}) copy-start(bf16[64,16,2048]{2,1,0:T(8,128)(2,1)} %param.20) | copy-start | bytes 12582916
  89.1 3.1 %copy-start.6 = (f32[128]{0:T(128)}, f32[128]{0:T(128)S(1)}, u32[]{:S(2)}) copy-start(f32[128]{0:T(128)S(1)} %get-tuple-element.104) | copy-start | bytes 1540
  92.2 6.3 %copy-start = (f32[1024,512]{0,1:T(8,128)}, f32[1024,512]{0,1:T(8,128)S(1)}, u32[]{:S(2)}) copy-start(f32[1024,512]{0,1:T(8,128)S(1)} %convolution_bitcast_fusion) | copy-start | bytes 6291460
  100.9 25.5 %all-to-all-start.2 = ((f32[128,4,128]{2,1,0:T(4,128)}), f32[128,4,128]{2,1,0:T(4,128)S(1)}, u32[]{:S(2)}, u32[]{:S(2)}) async-start(f32[128,4,128]{2,1,0:T(4,128)} %broadcast_in_dim.18), calls=%async_computation.2 | async-start | bytes 524288 | tf_op jit(solution)/shard_map/all_to_all | solution.py:25
  127.2 3.2 %collective-permute-start.8 = (f32[4,128]{1,0:T(4,128)S(1)}, f32[4,128]{1,0:T(4,128)S(1)}, u32[]{:S(2)}, u32[]{:S(2)}) collective-permute-start(f32[4,128]{1,0:T(4,128)S(1)} %slice.241), channel_id=1, source_target_pairs={{0,1},{1,0},{2,3},{3,2},{4,5},{5,4},{6,7},{7,6},{8,9},{9,8},{10,11... | collective-permute-start | bytes 6152 | tf_op jit(solution)/shard_map/ppermute | solution.py:74
  130.5 1.6 copy-start.1
  130.5 1.6 copy-start.7
  139.7 20.3 %copy-start.8 = (s32[8]{0:T(128)S(1)}, s32[8]{0:T(128)}, u32[]{:S(2)}) copy-start(s32[8]{0:T(128)} %pad_add_fusion.3) | copy-start | bytes 100
  160.2 2.4 %collective-permute-start.9 = (f32[4,128]{1,0:T(4,128)S(1)}, f32[4,128]{1,0:T(4,128)S(1)}, u32[]{:S(2)}, u32[]{:S(2)}) collective-permute-start(f32[4,128]{1,0:T(4,128)S(1)} %slice.247), channel_id=1, source_target_pairs={{0,1},{1,0},{2,3},{3,2},{4,5},{5,4},{6,7},{7,6},{8,9},{9,8},{10,11... | collective-permute-start | bytes 6152 | tf_op jit(solution)/shard_map/ppermute | solution.py:74

commit v2 on v1

v2 whole, which is shorter than its diff:
```python
import jax
import jax.numpy as jnp
from jax import lax
from jax.experimental import pallas as pl
from jax.experimental.pallas import tpu as pltpu
from jax.sharding import Mesh
from jax.sharding import PartitionSpec as P


BLK = 128
SLOTS = 4
WIDTH = SLOTS * BLK
NBLK = 32
EVERY = ("py_0", "py_1", "px_0", "px_1", "px_2")
PY = ("py_0", "py_1")
PX = ("px_0", "px_1", "px_2")
COLUMN = ("py_0", "py_1", "px_1")
PLANE = ("py_0", "py_1", "px_2", "px_0")
MATES = ("px_0", "py_1", "px_1", "py_0")
CORE = "px_2"
F32 = jnp.float32
BF16 = jnp.bfloat16
ROW_TILE = 512
VMEM_BYTES = 48 << 20


def to_everyone(value, axes):
    copies = jnp.broadcast_to(value[None], (lax.axis_size(axes), *value.shape))
    return lax.all_to_all(copies, axes, split_axis=0, concat_axis=0, tiled=True)


def swapped(value, axis, bits):
    return lax.ppermute(value, axis, [(i, i ^ bits) for i in range(lax.axis_size(axis))])


def in_place_order(value, dim, axis):
    size = value.shape[dim]
    at = lax.axis_index(axis)
    bit = 1
    while bit < size:
        shape = (*value.shape[:dim], size // (2 * bit), 2, bit, *value.shape[dim + 1 :])
        flipped = jnp.flip(value.reshape(shape), dim + 1).reshape(value.shape)
        value = jnp.where((at & bit) != 0, flipped, value)
        bit *= 2
    return value


def select_kernel(place_ref, *refs):
    *ids_refs, rows_ref, out_hbm, zero_ref, sem = refs
    zero_ref[...] = jnp.zeros_like(zero_ref)
    place = place_ref[0, 0]
    chunk = ids_refs[0].shape[0]
    for far, ids_ref in enumerate(ids_refs):

        @pl.loop(0, chunk)
        def _(near):
            tile = (far * chunk + near) ^ place
            for slot in range(SLOTS):
                block = ids_ref[near, slot]
                target = out_hbm.at[tile, slot]

                @pl.when(block < NBLK)
                def _():
                    lane = pl.multiple_of((block % SLOTS) * BLK, BLK)
                    source = rows_ref.at[block // SLOTS, :, :, pl.ds(lane, BLK)]
                    pltpu.make_async_copy(source, target, sem).start()

                @pl.when(block >= NBLK)
                def _():
                    pltpu.make_async_copy(zero_ref, target, sem).start()

    pltpu.make_async_copy(out_hbm, out_hbm, sem).wait()


def select(place, ids_pieces, rows):
    tiles = sum(piece.shape[0] for piece in ids_pieces)
    smem = pl.BlockSpec(memory_space=pltpu.SMEM)
    anywhere = pl.BlockSpec(memory_space=pltpu.HBM)
    return pl.pallas_call(
        select_kernel,
        out_shape=jax.ShapeDtypeStruct((tiles, SLOTS, *rows.shape[1:3], BLK), rows.dtype),
        in_specs=[smem] * (1 + len(ids_pieces)) + [pl.BlockSpec(memory_space=pltpu.VMEM)],
        out_specs=anywhere,
        scratch_shapes=[
            pltpu.VMEM((rows.shape[1], rows.shape[2], BLK), rows.dtype),
            pltpu.SemaphoreType.DMA,
        ],
        cost_estimate=pl.CostEstimate(flops=1 << 20, bytes_accessed=1 << 22, transcendentals=0),
        name="select",
    )(place, *ids_pieces, rows)


def sweep(a_ref, hi_ref, lo_ref, cross_ref, gram_ref, inv_ref, colsq_ref):
    pixels = a_ref.shape[0]
    for slot in range(SLOTS):
        c = slice(slot * BLK, (slot + 1) * BLK)
        weights = gram_ref[slot]
        total = jnp.zeros((1, BLK), F32)
        for low in range(0, pixels, ROW_TILE):
            r = slice(low, low + ROW_TILE)
            both = jnp.dot(hi_ref[r, :], weights, preferred_element_type=F32)
            both += jnp.dot(lo_ref[r, :], weights, preferred_element_type=F32)
            resid = cross_ref[r, c] - (both[:, :BLK] + both[:, BLK:])
            fresh = jnp.maximum(a_ref[r, c] + resid * inv_ref[:, c], 0.0)
            a_ref[r, c] = fresh
            if slot < SLOTS - 1:
                high = fresh.astype(BF16)
                hi_ref[r, c] = high
                lo_ref[r, c] = (fresh - high.astype(F32)).astype(BF16)
            total += jnp.sum(fresh * fresh, axis=0, keepdims=True)
        colsq_ref[slot : slot + 1, :] = total


def put_parts(value, r, a_ref, hi_ref, lo_ref):
    a_ref[r, :] = value
    high = value.astype(BF16)
    hi_ref[r, :] = high
    lo_ref[r, :] = (value - high.astype(F32)).astype(BF16)


def first_kernel(
    live_ref, recv_ref, movie_hbm, foot_hbm,
    a_ref, colsq_ref, cross_ref, gram_ref, inv_ref,
    movie_ref, foot_ref, picked_ref, square_ref, hi_ref, lo_ref, sems,
):
    copies = [
        pltpu.make_async_copy(source, target, sems.at[i])
        for i, (source, target) in enumerate(
            ((movie_hbm, movie_ref), (foot_hbm, foot_ref))
        )
    ]
    for copy in copies:
        copy.start()
    groups, cores, halves, _, depth, part, _ = recv_ref.shape
    base = 0
    for half in range(halves):
        for z in range(depth):
            for core in range(cores):
                size = groups * part
                for slot in range(SLOTS):
                    piece = recv_ref[:, core, half, slot, z].astype(F32).reshape(size, BLK)
                    picked_ref[base : base + size, slot * BLK : (slot + 1) * BLK] = piece.astype(BF16)
                base += size
    picked = picked_ref[...]
    square_ref[...] = lax.dot_general(
        picked, picked, (((0,), (0,)), ((), ())), preferred_element_type=F32
    )
    eye = lax.broadcasted_iota(jnp.int32, (BLK, BLK), 0) == lax.broadcasted_iota(
        jnp.int32, (BLK, BLK), 1
    )
    for slot in range(SLOTS):
        c = slice(slot * BLK, (slot + 1) * BLK)
        columns = square_ref[:, c]
        high = columns.astype(BF16)
        gram_ref[slot, :, :BLK] = high
        gram_ref[slot, :, BLK:] = (columns - high.astype(F32)).astype(BF16)
        diagonal = jnp.sum(jnp.where(eye, square_ref[c, c], 0.0), axis=0, keepdims=True)
        inv_ref[:, c] = 1.0 / (diagonal + 1e-06 + (1.0 - live_ref[:, c]))
    copies[0].wait()
    pixels = movie_ref.shape[0]
    for low in range(0, pixels, ROW_TILE):
        r = slice(low, low + ROW_TILE)
        cross_ref[r, :] = jnp.dot(movie_ref[r, :], picked, preferred_element_type=F32)
    copies[1].wait()
    for low in range(0, pixels, ROW_TILE):
        r = slice(low, low + ROW_TILE)
        put_parts(foot_ref[r, :] * live_ref[...], r, a_ref, hi_ref, lo_ref)
    sweep(a_ref, hi_ref, lo_ref, cross_ref, gram_ref, inv_ref, colsq_ref)


def second_kernel(
    scale_ref, old_ref, cross_ref, gram_ref, inv_ref, a_ref, colsq_ref, hi_ref, lo_ref
):
    for low in range(0, old_ref.shape[0], ROW_TILE):
        r = slice(low, low + ROW_TILE)
        put_parts(old_ref[r, :] * scale_ref[...], r, a_ref, hi_ref, lo_ref)
    sweep(a_ref, hi_ref, lo_ref, cross_ref, gram_ref, inv_ref, colsq_ref)


def first_pass(live, received, tile_movie, tile_foot):
    pixels, frames = tile_movie.shape
    vmem = pl.BlockSpec(memory_space=pltpu.VMEM)
    hbm = pl.BlockSpec(memory_space=pltpu.HBM)
    return pl.pallas_call(
        first_kernel,
        out_shape=(
            pltpu.VMEM((pixels, WIDTH), F32),
            pltpu.VMEM((SLOTS, BLK), F32),
            pltpu.VMEM((pixels, WIDTH), F32),
            pltpu.VMEM((SLOTS, WIDTH, 2 * BLK), BF16),
            pltpu.VMEM((1, WIDTH), F32),
        ),
        in_specs=[vmem, vmem, hbm, hbm],
        out_specs=(vmem,) * 5,
        scratch_shapes=[
            pltpu.VMEM(tile_movie.shape, tile_movie.dtype),
            pltpu.VMEM(tile_foot.shape, F32),
            pltpu.VMEM((frames, WIDTH), BF16),
            pltpu.VMEM((WIDTH, WIDTH), F32),
            pltpu.VMEM((pixels, WIDTH), BF16),
            pltpu.VMEM((pixels, WIDTH), BF16),
            pltpu.SemaphoreType.DMA((2,)),
        ],
        compiler_params=pltpu.CompilerParams(vmem_limit_bytes=VMEM_BYTES),
        cost_estimate=pl.CostEstimate(flops=7 << 30, bytes_accessed=12 << 20, transcendentals=0),
        name="first_pass",
    )(live, received, tile_movie, tile_foot)


def second_pass(scale, a, cross, gram, inv):
    pixels = a.shape[0]
    vmem = pl.BlockSpec(memory_space=pltpu.VMEM)
    return pl.pallas_call(
        second_kernel,
        out_shape=(pltpu.VMEM((pixels, WIDTH), F32), pltpu.VMEM((SLOTS, BLK), F32)),
        in_specs=[vmem] * 5,
        out_specs=(vmem,) * 2,
        scratch_shapes=[pltpu.VMEM((pixels, WIDTH), BF16), pltpu.VMEM((pixels, WIDTH), BF16)],
        compiler_params=pltpu.CompilerParams(vmem_limit_bytes=VMEM_BYTES // 2),
        cost_estimate=pl.CostEstimate(flops=4 << 30, bytes_accessed=8 << 20, transcendentals=0),
        name="second_pass",
    )(scale, a, cross, gram, inv)


def totals_of(colsq, match):
    seen = to_everyone(colsq, MATES).reshape(-1, BLK)
    sums = jnp.dot(match, seen, precision=lax.Precision.HIGHEST)
    return sums[:SLOTS] + swapped(sums[SLOTS:], CORE, 1)


def per_device(movie, traces, footprints, block_ids):
    rows, cols, frames = movie.shape
    pixels = rows * cols
    n_group = lax.axis_size(PY)
    n_z = lax.axis_size("px_1")
    sizes = {axis: lax.axis_size(axis) for axis in EVERY}
    part = traces.shape[1] // n_group
    my_ids = block_ids.reshape(SLOTS)

    pieces = traces.T.reshape(n_group, 1, part, traces.shape[0])
    pieces = jnp.broadcast_to(pieces, (n_group, n_z, part, traces.shape[0]))
    pieces = pieces.reshape(n_group * n_z, part, traces.shape[0])
    spread = lax.all_to_all(pieces, COLUMN, split_axis=0, concat_axis=0, tiled=True)
    spread = spread.reshape(n_group, n_z, part, traces.shape[0])
    spread = pltpu.with_memory_space_constraint(spread, pltpu.VMEM)

    other_half = swapped(my_ids[None], "px_0", 1)
    near = jnp.concatenate([my_ids[None], other_half])
    near = jnp.concatenate([near] + [swapped(near, ("py_1", CORE), bits) for bits in (1, 2, 3)])
    plane_ids = [near] + [swapped(near, "py_0", bits) for bits in (1, 2, 3)]
    place = lax.axis_index(PLANE).reshape(1, 1)
    outgoing = select(place, plane_ids, spread)
    outgoing, every_ids = lax.optimization_barrier((outgoing, jnp.concatenate(plane_ids)))
    received = lax.all_to_all(outgoing, PLANE, split_axis=0, concat_axis=0, tiled=True)
    received = received.reshape(n_group, sizes[CORE], sizes["px_0"], SLOTS, n_z, part, BLK)
    received = pltpu.with_memory_space_constraint(received, pltpu.VMEM)
    for bit in (1, 2, 4):
        far = swapped(every_ids, "px_1", bit)
        every_ids = jnp.concatenate([every_ids, far])
    mate_ids = every_ids.reshape(n_z, sizes["py_0"], sizes["py_1"], 2, sizes["px_0"], SLOTS)
    mate_ids = mate_ids[:, :, :, 0].transpose(3, 2, 0, 1, 4)
    for dim, axis in enumerate(MATES):
        mate_ids = in_place_order(mate_ids, dim, axis)
    wanted = jnp.concatenate([my_ids, near[2]])
    match = (wanted[:, None] == mate_ids.reshape(1, -1)).astype(F32)
    live = (my_ids < NBLK).astype(F32)
    column_live = jnp.repeat(live, BLK).reshape(1, WIDTH)
    column_live, match = lax.optimization_barrier((column_live, match))

    pixall = pixels * lax.axis_size(EVERY)
    tile_movie = pltpu.with_memory_space_constraint(movie.reshape(pixels, frames), pltpu.HBM)
    tile_foot = pltpu.with_memory_space_constraint(footprints.reshape(pixels, WIDTH), pltpu.HBM)
    current, colsq, cross, gram, inv = first_pass(column_live, received, tile_movie, tile_foot)
    current, cross = (pltpu.with_memory_space_constraint(x, pltpu.VMEM) for x in (current, cross))
    scale = live[:, None] / jnp.sqrt(totals_of(colsq, match) / pixall + 1e-06)
    current, colsq = second_pass(scale.reshape(1, WIDTH), current, cross, gram, inv)
    scale = live[:, None] / jnp.sqrt(totals_of(colsq, match) / pixall + 1e-06)
    return (current * scale.reshape(1, WIDTH)).reshape(rows, cols, WIDTH)


def solution(mesh):
    finer = Mesh(mesh.devices.reshape(4, 2, 2, 8, 2), EVERY)
    placed = (P(PY, PX, None), P(PY, PX), P(PY, PX, None), P(PY, PX, None))

    return jax.shard_map(
        per_device, mesh=finer, in_specs=placed, out_specs=P(PY, PX, None), check_vma=False
    )
```

time: 165 us -> 145 us (0.88)
  matrix products: 21.8 us -> 0.45 us
  blocking collectives: 20 us -> 37.1 us
  local copies, waits for them, and re-layouts: 17.2 us -> 5.45 us
  starting transfers between devices: 58 us -> 46.9 us
  Pallas kernels: 5.62 us -> 13.7 us
  other arithmetic: 10.8 us -> 3.68 us
  waiting for transfers between devices: 30.8 us -> 37.4 us
    dot_general x10 -> x0, matrix products: 20.8 us -> none  [the longest x8 14.9 us: per_device(): jnp.dot(current, gram[:, low:low + BLK], precision=lax.Precision.HIGHEST)]
    all_to_all x1, waiting for transfers between devices: 8.93 us -> 27.9 us  [per_device(): lax.all_to_all(outgoing, PLANE, split_axis=0, concat_axis=0, tiled=True)]
    all_to_all x1 -> x2, blocking collectives: 20 us -> 37.1 us  [to_everyone(): return lax.all_to_all(copies, axes, split_axis=0, concat_axis=0, tiled=True)]
    all_to_all x1 -> x0, starting transfers between devices: 11.7 us -> none  [to_everyone(): return lax.all_to_all(copies, axes, split_axis=0, concat_axis=0, tiled=True)]
    all_to_all x1 -> x0, waiting for transfers between devices: 11.1 us -> none  [to_everyone(): return lax.all_to_all(copies, axes, split_axis=0, concat_axis=0, tiled=True)]
    pallas_call x1 -> x3, Pallas kernels: 5.62 us -> 13.7 us  [the longest x1 8.09 us: first_pass(): pl.pallas_call(first_kernel, out_shape=(pltpu.VMEM((pixels, WIDTH), F32),...]
    reshape x2 -> x0, local copies, waits for them, and re-layouts: 3.82 us -> none  [the longest x1 2.01 us: per_device(): picked = received.reshape(n_group, sizes[2], sizes[4], n_z, part, WIDTH)]
    concatenate x6 -> x3, local copies, waits for them, and re-layouts: 3.54 us -> 0.91 us  [the longest x1 0.67 us: per_device(): jnp.concatenate([near] + [swapped(near, ('py_1', CORE), bits) for bits in...]
  transfers between devices with their start and end apart: 13 -> 14, of which waited for: 12 -> 10; matrix products, arithmetic and copies ran while one was open for 9% -> 4% of each run, Pallas kernels for 0% -> 0%
where the time goes in v2:
time: 145 us
  starting transfers between devices  46.9 us (32%)
  waiting for transfers between devices  37.4 us (26%)
  blocking collectives  37.1 us (26%)
  Pallas kernels  13.7 us (9%)
  local copies, waits for them, and re-layouts  5.45 us (4%)
  other arithmetic  3.68 us (3%)
    all_to_all x2, blocking collectives, to_everyone(): return lax.all_to_all(copies, axes, split_axis=0, concat_axis=0, tiled=True)  37.1 us
    all_to_all x1, waiting for transfers between devices, per_device(): lax.all_to_all(outgoing, PLANE, split_axis=0, concat_axis=0, tiled=True)  27.9 us
    ppermute x12, starting transfers between devices, swapped(): lax.ppermute(value, axis, [(i, i ^ bits) for i in range(lax.axis_size(axi...  23.8 us
    all_to_all x1, starting transfers between devices, per_device(): lax.all_to_all(pieces, COLUMN, split_axis=0, concat_axis=0, tiled=True)  13.5 us
    all_to_all x1, starting transfers between devices, per_device(): lax.all_to_all(outgoing, PLANE, split_axis=0, concat_axis=0, tiled=True)  9.61 us
    ppermute x12, waiting for transfers between devices, swapped(): lax.ppermute(value, axis, [(i, i ^ bits) for i in range(lax.axis_size(axi...  9.57 us
    pallas_call x1, Pallas kernels, first_pass(): pl.pallas_call(first_kernel, out_shape=(pltpu.VMEM((pixels, WIDTH), F32),...  8.09 us
  transfers between devices with their start and end apart: 14, of which 10 were waited for; matrix products, arithmetic and copies ran while one was open for 4% of the time, Pallas kernels for 0%

profile of v2, /device:TPU:1, one launch (start us, length us, event | category | flops | bytes accessed | tf_op | source)
XLA Modules:
  0.0 145.0 jit_solution(17863862246362350373)
XLA Ops:
  0.0 1.7 %broadcast_in_dim.9 = bf16[8,8,8,512]{3,2,1,0:T(8,128)(2,1)} broadcast(bf16[8,8,512]{2,1,0:T(8,128)(2,1)} %bitcast.59), dimensions={0,2,3} | broadcast | bytes 589824 | tf_op jit(solution)/shard_map/broadcast_in_dim | solution.py:241
  1.7 13.5 %all-to-all-start = ((bf16[64,8,512]{2,1,0:T(8,128)(2,1)}), bf16[64,8,512]{2,1,0:T(8,128)(2,1)S(1)}, u32[]{:S(2)}, u32[]{:S(2)}) async-start(bf16[64,8,512]{2,1,0:T(8,128)(2,1)} %bitcast.7), calls=%async_computation | async-start | bytes 1048576 | tf_op jit(solution)/shard_map/all_to_all | solution.py:243
  15.2 2.7 %collective-permute-start = (s32[1,4]{1,0:T(1,128)}, s32[1,4]{1,0:T(1,128)S(1)}, u32[]{:S(2)}, u32[]{:S(2)}) collective-permute-start(s32[1,4]{1,0:T(1,128)} %bitcast.60), channel_id=1, source_target_pairs={{0,16},{16,0},{1,17},{17,1},{2,18},{18,2},{3,19},{19,3},{4,20},{20... | collective-permute-start | bytes 56 | tf_op jit(solution)/shard_map/ppermute | solution.py:33
  17.9 0.8 copy.15
  18.7 0.7 compare_convert_fusion.1
  19.3 0.1 collective-permute-done
  19.4 0.7 pad_add_fusion.3
  20.0 3.2 %collective-permute-start.3 = (s32[2,4]{1,0:T(2,128)S(1)}, s32[2,4]{1,0:T(2,128)S(1)}, u32[]{:S(2)}, u32[]{:S(2)}) collective-permute-start(s32[2,4]{1,0:T(2,128)S(1)} %pad_add_fusion.3), channel_id=1, source_target_pairs={{0,33},{1,32},{32,1},{33,0},{2,35},{3,34},{34,3},{35,2},{4,37},{5,... | collective-permute-start | bytes 104 | tf_op jit(solution)/shard_map/ppermute | solution.py:33
  23.3 0.2 collective-permute-start.2
  23.4 0.3 collective-permute-start.1
  23.8 0.1 copy.16
  23.9 1.0 collective-permute-done.3
  24.9 1.1 collective-permute-done.2
  26.0 0.0 collective-permute-done.1
  26.0 0.7 concatenate.27.refs_0_
  26.7 2.7 %collective-permute-start.6 = (s32[8,4]{1,0:T(8,128)S(1)}, s32[8,4]{1,0:T(8,128)S(1)}, u32[]{:S(2)}, u32[]{:S(2)}) collective-permute-start(s32[8,4]{1,0:T(8,128)S(1)} %concatenate.27.refs_0_), channel_id=1, source_target_pairs={{0,192},{64,128},{128,64},{192,0},{1,193},{65,129},{129,65},{193,1... | collective-permute-start | bytes 392 | tf_op jit(solution)/shard_map/ppermute | solution.py:33
  29.4 0.4 collective-permute-start.5
  29.8 0.3 collective-permute-start.4
  30.1 0.1 copy.19
  30.2 0.1 copy.18
  30.3 0.1 copy.17
  30.4 0.4 collective-permute-done.6.refs_3_
  30.8 0.1 copy.22
  30.8 2.8 %collective-permute-done.5.refs_2_ = s32[8,4]{1,0:T(8,128)S(1)} collective-permute-done((s32[8,4]{1,0:T(8,128)S(1)}, s32[8,4]{1,0:T(8,128)S(1)}, u32[]{:S(2)}, u32[]{:S(2)}) %collective-permute-start.5) | collective-permute-done | bytes 160 | tf_op jit(solution)/shard_map/ppermute | solution.py:33
  33.7 0.1 copy.21
  33.8 0.0 collective-permute-done.4.refs_1_
  33.8 0.1 copy.20
  33.8 0.1 concatenate.28
  33.9 0.0 all-to-all-done
  33.9 0.0 copy-done
  34.0 0.0 copy-done.1
  34.0 0.3 copy-done.2
  34.3 0.1 copy-done.3
  34.3 2.9 %select.1 = bf16[32,4,8,8,128]{4,3,2,1,0:T(8,128)(2,1)} custom-call(s32[1,1]{1,0:T(1,128)} %bitcast.4.place_ref, s32[8,4]{1,0:T(8,128)} %copy-done, s32[8,4]{1,0:T(8,128)} %copy-done.3, s32[8,4]{1,0:T(8,128)} %copy-done.2, s32[8,4]{1,0:T(8,128)} %copy-done.1, bf16[8,8,8,512]{3,2,1,0:T(8,128)(2,1)S(1)} %bitcast.46), custom_call_target="tpu_custom_call" | custom-call | flops 1048576 | bytes 4194304 | tf_op jit(solution)/shard_map/select/pallas_call | solution.py:79
  37.2 1.3 collective-permute-start.7
  38.5 1.2 collective-permute-done.7
  39.7 0.1 pad_add_fusion.1
  39.8 2.1 %collective-permute-start.8 = (s32[64,4]{0,1:T(4,128)S(1)}, s32[64,4]{0,1:T(4,128)S(1)}, u32[]{:S(2)}, u32[]{:S(2)}) collective-permute-start(s32[64,4]{0,1:T(4,128)S(1)} %pad_add_fusion.1), channel_id=1, source_target_pairs={{0,4},{2,6},{4,0},{6,2},{8,12},{10,14},{12,8},{14,10},{1,5},{3,7},... | collective-permute-start | bytes 3080 | tf_op jit(solution)/shard_map/ppermute | solution.py:33
  41.9 1.2 collective-permute-done.8
  43.2 0.1 pad_add_fusion.2
  43.2 4.9 %collective-permute-start.9 = (s32[128,4]{0,1:T(4,128)S(1)}, s32[128,4]{0,1:T(4,128)S(1)}, u32[]{:S(2)}, u32[]{:S(2)}) collective-permute-start(s32[128,4]{0,1:T(4,128)S(1)} %pad_add_fusion.2), channel_id=1, source_target_pairs={{0,8},{2,10},{4,12},{6,14},{8,0},{10,2},{12,4},{14,6},{1,9},{3,11}... | collective-permute-start | bytes 6152 | tf_op jit(solution)/shard_map/ppermute | solution.py:33
  48.1 0.1 pad_add_fusion.4
  48.2 9.6 %all-to-all-start.1 = ((bf16[32,4,8,8,128]{4,3,2,1,0:T(8,128)(2,1)}), bf16[32,4,8,8,128]{4,3,2,1,0:T(8,128)(2,1)S(1)}, u32[]{:S(2)}, u32[]{:S(2)}) async-start(bf16[32,4,8,8,128]{4,3,2,1,0:T(8,128)(2,1)} %select.1), calls=%async_computation.1 | async-start | bytes 4194304 | tf_op jit(solution)/shard_map/all_to_all | solution.py:254
  57.8 0.0 collective-permute-done.9
  57.8 0.1 pad_add_fusion
  57.9 0.1 copy.23
  58.1 0.2 reshape.98
  58.7 0.1 eq.16
  58.8 0.1 compare_convert_fusion
  58.9 0.6 div.20
  59.5 27.9 %all-to-all-done.1 = bf16[32,4,8,8,128]{4,3,2,1,0:T(8,128)(2,1)S(1)} async-done(((bf16[32,4,8,8,128]{4,3,2,1,0:T(8,128)(2,1)}), bf16[32,4,8,8,128]{4,3,2,1,0:T(8,128)(2,1)S(1)}, u32[]{:S(2)}, u32[]{:S(2)}) %all-to-all-start.1) | async-done | bytes 2097184 | tf_op jit(solution)/shard_map/all_to_all | solution.py:254
  87.4 8.1 %first_pass.1 = (f32[1024,512]{1,0:T(8,128)S(1)}, f32[4,128]{1,0:T(4,128)S(1)}, f32[1024,512]{1,0:T(8,128)S(1)}, bf16[4,512,256]{2,1,0:T(8,128)(2,1)S(1)}, f32[1,512]{1,0:T(1,128)S(1)}) custom-call(f32[1,512]{1,0:T(1,128)} %bitcast.65, bf16[8,2,2,4,8,8,128]{6,5,4,3,2,1,0:T(8,128)(2,1)S(1)} %bitcast.45, bf16[1024,2048]{1,0:T(8,128)(2,1)} %bitcast.66, ...), custom_call_target="tpu_custom_call" | custom-call | flops 7516192768 | bytes 12582912 | tf_op jit(solution)/shard_map/first_pass/pallas_call | solution.py:184
  95.5 18.4 %all_to_all.20 = f32[128,4,128]{2,1,0:T(4,128)S(1)} all-to-all(f32[128,4,128]{2,1,0:T(4,128)S(1)} %broadcast_in_dim.10), channel_id=1, replica_groups=mesh['py_0'=4,'py_1'=2,'px_0'=2,'px_1'=8,'px_2'=2] {'px_0','py_1','px_1'..., dimensions={0} | all-to-all | bytes 524288 | tf_op jit(solution)/shard_map/all_to_all | solution.py:29
  113.9 0.2 fusion
  114.1 3.1 %collective-permute-start.10 = (f32[4,128]{1,0:T(4,128)S(1)}, f32[4,128]{1,0:T(4,128)S(1)}, u32[]{:S(2)}, u32[]{:S(2)}) collective-permute-start(f32[4,128]{1,0:T(4,128)S(1)} %slice.21), channel_id=1, source_target_pairs={{0,1},{1,0},{2,3},{3,2},{4,5},{5,4},{6,7},{7,6},{8,9},{9,8},{10,11... | collective-permute-start | bytes 6152 | tf_op jit(solution)/shard_map/ppermute | solution.py:33
  117.2 0.8 collective-permute-done.10
  118.1 0.1 rsqrt_multiply_fusion
  118.1 2.8 %second_pass.1 = (f32[1024,512]{1,0:T(8,128)S(1)}, f32[4,128]{1,0:T(4,128)S(1)}) custom-call(f32[1,512]{1,0:T(1,128)S(1)} %bitcast.47, f32[1024,512]{1,0:T(8,128)S(1)} %get-tuple-element.21.old_ref, f32[1024,512]{1,0:T(8,128)S(1)} %get-tuple-element.22.cross_ref, bf16[4,512,256]{2,1,0:T(8,128)(2,1)S(1)} %get-tuple-element.23.gram_ref, ...), custom_call_target="tpu_custom_call" | custom-call | flops 4294967296 | bytes 8388608 | tf_op jit(solution)/shard_map/second_pass/pallas_call | solution.py:213
  120.9 18.7 %all_to_all.21 = f32[128,4,128]{2,1,0:T(4,128)S(1)} all-to-all(f32[128,4,128]{2,1,0:T(4,128)S(1)} %broadcast_in_dim.11), channel_id=1, replica_groups=mesh['py_0'=4,'py_1'=2,'px_0'=2,'px_1'=8,'px_2'=2] {'px_0','py_1','px_1'..., dimensions={0} | all-to-all | bytes 524288 | tf_op jit(solution)/shard_map/all_to_all | solution.py:29
  139.6 0.2 fusion.1
  139.9 2.7 %collective-permute-start.11 = (f32[4,128]{1,0:T(4,128)S(1)}, f32[4,128]{1,0:T(4,128)S(1)}, u32[]{:S(2)}, u32[]{:S(2)}) collective-permute-start(f32[4,128]{1,0:T(4,128)S(1)} %slice.23), channel_id=1, source_target_pairs={{0,1},{1,0},{2,3},{3,2},{4,5},{5,4},{6,7},{7,6},{8,9},{9,8},{10,11... | collective-permute-start | bytes 6152 | tf_op jit(solution)/shard_map/ppermute | solution.py:33
  142.5 0.8 collective-permute-done.11
  143.4 0.1 multiply_bitcast_fusion
  143.4 1.6 %broadcast_multiply_fusion = f32[1024,512]{1,0:T(8,128)} fusion(f32[1024,512]{1,0:T(8,128)S(1)} %get-tuple-element.25, f32[512]{0:T(512)S(1)} %multiply_bitcast_fusion), kind=kLoop, calls=%fused_computation | loop fusion | flops 524288 | bytes 4196352 | tf_op jit(solution)/shard_map/mul | solution.py:278
  (25 shorter events, 0.5 us)
Async XLA Ops:
  0.0 48.1 %copy-start.4 = (s32[1,1,4]{2,1,0:T(1,128)S(1)}, s32[1,1,4]{2,1,0:T(1,128)}, u32[]{:S(2)}) copy-start(s32[1,1,4]{2,1,0:T(1,128)} %param.7) | copy-start | bytes 52
  1.7 32.3 %all-to-all-start = ((bf16[64,8,512]{2,1,0:T(8,128)(2,1)}), bf16[64,8,512]{2,1,0:T(8,128)(2,1)S(1)}, u32[]{:S(2)}, u32[]{:S(2)}) async-start(bf16[64,8,512]{2,1,0:T(8,128)(2,1)} %bitcast.7), calls=%async_computation | async-start | bytes 1048576 | tf_op jit(solution)/shard_map/all_to_all | solution.py:243
  15.2 4.2 %collective-permute-start = (s32[1,4]{1,0:T(1,128)}, s32[1,4]{1,0:T(1,128)S(1)}, u32[]{:S(2)}, u32[]{:S(2)}) collective-permute-start(s32[1,4]{1,0:T(1,128)} %bitcast.60), channel_id=1, source_target_pairs={{0,16},{16,0},{1,17},{17,1},{2,18},{18,2},{3,19},{19,3},{4,20},{20... | collective-permute-start | bytes 56 | tf_op jit(solution)/shard_map/ppermute | solution.py:33
  20.0 4.8 %collective-permute-start.3 = (s32[2,4]{1,0:T(2,128)S(1)}, s32[2,4]{1,0:T(2,128)S(1)}, u32[]{:S(2)}, u32[]{:S(2)}) collective-permute-start(s32[2,4]{1,0:T(2,128)S(1)} %pad_add_fusion.3), channel_id=1, source_target_pairs={{0,33},{1,32},{32,1},{33,0},{2,35},{3,34},{34,3},{35,2},{4,37},{5,... | collective-permute-start | bytes 104 | tf_op jit(solution)/shard_map/ppermute | solution.py:33
  23.3 2.7 %collective-permute-start.2 = (s32[2,4]{1,0:T(2,128)S(1)}, s32[2,4]{1,0:T(2,128)S(1)}, u32[]{:S(2)}, u32[]{:S(2)}) collective-permute-start(s32[2,4]{1,0:T(2,128)S(1)} %pad_add_fusion.3), channel_id=1, source_target_pairs={{0,32},{1,33},{32,0},{33,1},{2,34},{3,35},{34,2},{35,3},{4,36},{5,... | collective-permute-start | bytes 104 | tf_op jit(solution)/shard_map/ppermute | solution.py:33
  23.4 2.6 %collective-permute-start.1 = (s32[2,4]{1,0:T(2,128)S(1)}, s32[2,4]{1,0:T(2,128)S(1)}, u32[]{:S(2)}, u32[]{:S(2)}) collective-permute-start(s32[2,4]{1,0:T(2,128)S(1)} %pad_add_fusion.3), channel_id=1, source_target_pairs={{0,1},{1,0},{32,33},{33,32},{2,3},{3,2},{34,35},{35,34},{4,5},{5,4... | collective-permute-start | bytes 104 | tf_op jit(solution)/shard_map/ppermute | solution.py:33
  26.7 7.3 %copy-start = (s32[8,4]{1,0:T(8,128)}, s32[8,4]{1,0:T(8,128)S(1)}, u32[]{:S(2)}) copy-start(s32[8,4]{1,0:T(8,128)S(1)} %concatenate.27.refs_0_) | copy-start | bytes 388
  26.7 4.1 %collective-permute-start.6 = (s32[8,4]{1,0:T(8,128)S(1)}, s32[8,4]{1,0:T(8,128)S(1)}, u32[]{:S(2)}, u32[]{:S(2)}) collective-permute-start(s32[8,4]{1,0:T(8,128)S(1)} %concatenate.27.refs_0_), channel_id=1, source_target_pairs={{0,192},{64,128},{128,64},{192,0},{1,193},{65,129},{129,65},{193,1... | collective-permute-start | bytes 392 | tf_op jit(solution)/shard_map/ppermute | solution.py:33
  29.4 4.3 %collective-permute-start.5 = (s32[8,4]{1,0:T(8,128)S(1)}, s32[8,4]{1,0:T(8,128)S(1)}, u32[]{:S(2)}, u32[]{:S(2)}) collective-permute-start(s32[8,4]{1,0:T(8,128)S(1)} %concatenate.27.refs_0_), channel_id=1, source_target_pairs={{0,128},{64,192},{128,0},{192,64},{1,129},{65,193},{129,1},{193,65... | collective-permute-start | bytes 392 | tf_op jit(solution)/shard_map/ppermute | solution.py:33
  29.8 4.0 %collective-permute-start.4 = (s32[8,4]{1,0:T(8,128)S(1)}, s32[8,4]{1,0:T(8,128)S(1)}, u32[]{:S(2)}, u32[]{:S(2)}) collective-permute-start(s32[8,4]{1,0:T(8,128)S(1)} %concatenate.27.refs_0_), channel_id=1, source_target_pairs={{0,64},{64,0},{128,192},{192,128},{1,65},{65,1},{129,193},{193,129... | collective-permute-start | bytes 392 | tf_op jit(solution)/shard_map/ppermute | solution.py:33
  30.8 3.2 %copy-start.1 = (s32[8,4]{1,0:T(8,128)}, s32[8,4]{1,0:T(8,128)S(1)}, u32[]{:S(2)}) copy-start(s32[8,4]{1,0:T(8,128)S(1)} %collective-permute-done.6.refs_3_) | copy-start | bytes 388
  33.7 0.6 copy-start.2
  33.8 0.6 copy-start.3
  37.2 2.5 %collective-permute-start.7 = (s32[32,4]{0,1:T(4,128)S(1)}, s32[32,4]{0,1:T(4,128)S(1)}, u32[]{:S(2)}, u32[]{:S(2)}) collective-permute-start(s32[32,4]{0,1:T(4,128)S(1)} %concatenate.28), channel_id=1, source_target_pairs={{0,2},{2,0},{4,6},{6,4},{8,10},{10,8},{12,14},{14,12},{1,3},{3,1},... | collective-permute-start | bytes 1544 | tf_op jit(solution)/shard_map/ppermute | solution.py:33
  39.8 3.4 %collective-permute-start.8 = (s32[64,4]{0,1:T(4,128)S(1)}, s32[64,4]{0,1:T(4,128)S(1)}, u32[]{:S(2)}, u32[]{:S(2)}) collective-permute-start(s32[64,4]{0,1:T(4,128)S(1)} %pad_add_fusion.1), channel_id=1, source_target_pairs={{0,4},{2,6},{4,0},{6,2},{8,12},{10,14},{12,8},{14,10},{1,5},{3,7},... | collective-permute-start | bytes 3080 | tf_op jit(solution)/shard_map/ppermute | solution.py:33
  43.2 14.6 %collective-permute-start.9 = (s32[128,4]{0,1:T(4,128)S(1)}, s32[128,4]{0,1:T(4,128)S(1)}, u32[]{:S(2)}, u32[]{:S(2)}) collective-permute-start(s32[128,4]{0,1:T(4,128)S(1)} %pad_add_fusion.2), channel_id=1, source_target_pairs={{0,8},{2,10},{4,12},{6,14},{8,0},{10,2},{12,4},{14,6},{1,9},{3,11}... | collective-permute-start | bytes 6152 | tf_op jit(solution)/shard_map/ppermute | solution.py:33
  48.2 39.2 %all-to-all-start.1 = ((bf16[32,4,8,8,128]{4,3,2,1,0:T(8,128)(2,1)}), bf16[32,4,8,8,128]{4,3,2,1,0:T(8,128)(2,1)S(1)}, u32[]{:S(2)}, u32[]{:S(2)}) async-start(bf16[32,4,8,8,128]{4,3,2,1,0:T(8,128)(2,1)} %select.1), calls=%async_computation.1 | async-start | bytes 4194304 | tf_op jit(solution)/shard_map/all_to_all | solution.py:254
  114.1 3.9 %collective-permute-start.10 = (f32[4,128]{1,0:T(4,128)S(1)}, f32[4,128]{1,0:T(4,128)S(1)}, u32[]{:S(2)}, u32[]{:S(2)}) collective-permute-start(f32[4,128]{1,0:T(4,128)S(1)} %slice.21), channel_id=1, source_target_pairs={{0,1},{1,0},{2,3},{3,2},{4,5},{5,4},{6,7},{7,6},{8,9},{9,8},{10,11... | collective-permute-start | bytes 6152 | tf_op jit(solution)/shard_map/ppermute | solution.py:33
  139.9 3.5 %collective-permute-start.11 = (f32[4,128]{1,0:T(4,128)S(1)}, f32[4,128]{1,0:T(4,128)S(1)}, u32[]{:S(2)}, u32[]{:S(2)}) collective-permute-start(f32[4,128]{1,0:T(4,128)S(1)} %slice.23), channel_id=1, source_target_pairs={{0,1},{1,0},{2,3},{3,2},{4,5},{5,4},{6,7},{7,6},{8,9},{9,8},{10,11... | collective-permute-start | bytes 6152 | tf_op jit(solution)/shard_map/ppermute | solution.py:33

commit v3 on v2

v3 whole, which is shorter than its diff:
```python
import jax
import jax.numpy as jnp
from jax import lax
from jax.experimental import pallas as pl
from jax.experimental.pallas import tpu as pltpu
from jax.sharding import Mesh
from jax.sharding import PartitionSpec as P


BLK = 128
SLOTS = 4
WIDTH = SLOTS * BLK
NBLK = 32
EVERY = ("py_0", "py_1", "px_0", "px_1", "px_2")
PY = ("py_0", "py_1")
PX = ("px_0", "px_1", "px_2")
COLUMN = ("py_0", "py_1", "px_1")
PLANE = ("py_0", "py_1", "px_2", "px_0")
MATES = ("px_0", "py_1", "px_1", "py_0")
CORE = "px_2"
F32 = jnp.float32
BF16 = jnp.bfloat16
ROW_TILE = 512
VMEM_BYTES = 24 << 20


def to_everyone(value, axes):
    copies = jnp.broadcast_to(value[None], (lax.axis_size(axes), *value.shape))
    return lax.all_to_all(copies, axes, split_axis=0, concat_axis=0, tiled=True)


def swapped(value, axis, bits):
    return lax.ppermute(value, axis, [(i, i ^ bits) for i in range(lax.axis_size(axis))])


def in_place_order(value, dim, axis):
    size = value.shape[dim]
    at = lax.axis_index(axis)
    bit = 1
    while bit < size:
        shape = (*value.shape[:dim], size // (2 * bit), 2, bit, *value.shape[dim + 1 :])
        flipped = jnp.flip(value.reshape(shape), dim + 1).reshape(value.shape)
        value = jnp.where((at & bit) != 0, flipped, value)
        bit *= 2
    return value


def select_kernel(place_ref, *refs):
    *ids_refs, rows_ref, out_hbm, sem = refs
    place = place_ref[0, 0]
    chunk = ids_refs[0].shape[0]
    depth = rows_ref.shape[0] // (NBLK // SLOTS)
    for far, ids_ref in enumerate(ids_refs):

        @pl.loop(0, chunk, unroll=True)
        def _(near):
            tile = (far * chunk + near) ^ place
            for slot in range(SLOTS):
                block = jnp.minimum(ids_ref[near, slot], NBLK - 1)
                group = pl.multiple_of((block // SLOTS) * depth, depth)
                lane = pl.multiple_of((block % SLOTS) * BLK, BLK)
                pltpu.make_async_copy(
                    rows_ref.at[pl.ds(group, depth), :, pl.ds(lane, BLK)],
                    out_hbm.at[tile, slot],
                    sem,
                ).start()

    pltpu.make_async_copy(out_hbm, out_hbm, sem).wait()


def select(place, ids_pieces, rows):
    depth = rows.shape[0] // (NBLK // SLOTS)
    tiles = sum(piece.shape[0] for piece in ids_pieces)
    smem = pl.BlockSpec(memory_space=pltpu.SMEM)
    anywhere = pl.BlockSpec(memory_space=pltpu.HBM)
    return pl.pallas_call(
        select_kernel,
        out_shape=jax.ShapeDtypeStruct((tiles, SLOTS, depth, rows.shape[1], BLK), rows.dtype),
        in_specs=[smem] * (1 + len(ids_pieces)) + [pl.BlockSpec(memory_space=pltpu.VMEM)],
        out_specs=anywhere,
        scratch_shapes=[
            pltpu.SemaphoreType.DMA,
        ],
        cost_estimate=pl.CostEstimate(flops=1 << 20, bytes_accessed=1 << 22, transcendentals=0),
        compiler_params=pltpu.CompilerParams(vmem_limit_bytes=2 << 20),
        name="select",
    )(place, *ids_pieces, rows)


def sweep(base, a_ref, hi_ref, lo_ref, cross_ref, gram_ref, inv_ref, colsq_ref):
    pixels = a_ref.shape[0]
    for slot in range(SLOTS):
        c = slice(slot * BLK, (slot + 1) * BLK)
        weights = gram_ref[slot]
        total = jnp.zeros((1, BLK), F32)
        for low in range(0, pixels, ROW_TILE):
            r = slice(low, low + ROW_TILE)
            both = jnp.dot(hi_ref[r, :], weights, preferred_element_type=F32)
            both += jnp.dot(lo_ref[r, :], weights, preferred_element_type=F32)
            resid = cross_ref[r, c] - (both[:, :BLK] + both[:, BLK:])
            fresh = jnp.maximum(base(r, c) + resid * inv_ref[:, c], 0.0)
            a_ref[r, c] = fresh
            if slot < SLOTS - 1:
                high = fresh.astype(BF16)
                hi_ref[r, c] = high
                lo_ref[r, c] = (fresh - high.astype(F32)).astype(BF16)
            total += jnp.sum(fresh * fresh, axis=0, keepdims=True)
        colsq_ref[slot : slot + 1, :] = total


def put_parts(value, r, hi_ref, lo_ref):
    high = value.astype(BF16)
    hi_ref[r, :] = high
    lo_ref[r, :] = (value - high.astype(F32)).astype(BF16)


def first_kernel(
    ids_ref, live_ref, recv_ref, movie_hbm, foot_hbm,
    a_ref, colsq_ref, cross_ref, gram_ref, inv_ref,
    movie_ref, foot_ref, picked_ref, square_ref, hi_ref, lo_ref, sems,
):
    pixels = movie_ref.shape[0]
    tiles = [slice(low, low + ROW_TILE) for low in range(0, pixels, ROW_TILE)]
    movies = [
        pltpu.make_async_copy(movie_hbm.at[r, :], movie_ref.at[r, :], sems.at[i])
        for i, r in enumerate(tiles)
    ]
    foots = [
        pltpu.make_async_copy(foot_hbm.at[r, :], foot_ref.at[r, :], sems.at[len(tiles) + i])
        for i, r in enumerate(tiles)
    ]
    for copy in movies + foots:
        copy.start()
    groups, cores, halves, _, depth, part, _ = recv_ref.shape
    size = groups * part
    base = 0
    for half in range(halves):
        for z in range(depth):
            for core in range(cores):
                for slot in range(SLOTS):
                    piece = recv_ref[:, core, half, slot, z].astype(F32).reshape(size, BLK)
                    picked_ref[base : base + size, slot * BLK : (slot + 1) * BLK] = piece.astype(BF16)
                base += size
    for slot in range(SLOTS):

        @pl.when(ids_ref[0, slot] >= NBLK)
        def _():
            picked_ref[:, slot * BLK : (slot + 1) * BLK] = jnp.zeros((picked_ref.shape[0], BLK), BF16)

    picked = picked_ref[...]
    square_ref[...] = lax.dot_general(
        picked, picked, (((0,), (0,)), ((), ())), preferred_element_type=F32
    )
    eye = lax.broadcasted_iota(jnp.int32, (BLK, BLK), 0) == lax.broadcasted_iota(
        jnp.int32, (BLK, BLK), 1
    )
    for slot in range(SLOTS):
        c = slice(slot * BLK, (slot + 1) * BLK)
        columns = square_ref[:, c]
        high = columns.astype(BF16)
        gram_ref[slot, :, :BLK] = high
        gram_ref[slot, :, BLK:] = (columns - high.astype(F32)).astype(BF16)
        diagonal = jnp.sum(jnp.where(eye, square_ref[c, c], 0.0), axis=0, keepdims=True)
        inv_ref[:, c] = 1.0 / (diagonal + 1e-06 + (1.0 - live_ref[:, c]))
    for r, copy in zip(tiles, movies):
        copy.wait()
        cross_ref[r, :] = jnp.dot(movie_ref[r, :], picked, preferred_element_type=F32)
    for r, copy in zip(tiles, foots):
        copy.wait()
        put_parts(foot_ref[r, :] * live_ref[...], r, hi_ref, lo_ref)
    sweep(
        lambda r, c: foot_ref[r, c] * live_ref[:, c],
        a_ref, hi_ref, lo_ref, cross_ref, gram_ref, inv_ref, colsq_ref,
    )


def second_kernel(
    scale_ref, old_ref, cross_ref, gram_ref, inv_ref, a_ref, colsq_ref, hi_ref, lo_ref
):
    for low in range(0, old_ref.shape[0], ROW_TILE):
        r = slice(low, low + ROW_TILE)
        put_parts(old_ref[r, :] * scale_ref[...], r, hi_ref, lo_ref)
    sweep(
        lambda r, c: old_ref[r, c] * scale_ref[:, c],
        a_ref, hi_ref, lo_ref, cross_ref, gram_ref, inv_ref, colsq_ref,
    )


def last_kernel(scale_ref, a_ref, out_hbm, buffer_ref, sems):
    step = buffer_ref.shape[0] // sems.shape[0]
    copies = []
    for i in range(sems.shape[0]):
        r = slice(i * step, (i + 1) * step)
        buffer_ref[r, :] = a_ref[r, :] * scale_ref[...]
        copy = pltpu.make_async_copy(buffer_ref.at[r, :], out_hbm.at[r, :], sems.at[i])
        copy.start()
        copies.append(copy)
    for copy in copies:
        copy.wait()


VMEM_SPEC = pl.BlockSpec(memory_space=pltpu.VMEM)
HBM_SPEC = pl.BlockSpec(memory_space=pltpu.HBM)
SMEM_SPEC = pl.BlockSpec(memory_space=pltpu.SMEM)


def first_pass(ids, live, received, tile_movie, tile_foot):
    pixels, frames = tile_movie.shape
    return pl.pallas_call(
        first_kernel,
        out_shape=(
            pltpu.VMEM((pixels, WIDTH), F32),
            pltpu.VMEM((SLOTS, BLK), F32),
            pltpu.VMEM((pixels, WIDTH), F32),
            pltpu.VMEM((SLOTS, WIDTH, 2 * BLK), BF16),
            pltpu.VMEM((1, WIDTH), F32),
        ),
        in_specs=[SMEM_SPEC] + [VMEM_SPEC] * 2 + [HBM_SPEC] * 2,
        out_specs=(VMEM_SPEC,) * 5,
        scratch_shapes=[
            pltpu.VMEM((pixels, frames), BF16),
            pltpu.VMEM((pixels, WIDTH), F32),
            pltpu.VMEM((frames, WIDTH), BF16),
            pltpu.VMEM((WIDTH, WIDTH), F32),
            pltpu.VMEM((pixels, WIDTH), BF16),
            pltpu.VMEM((pixels, WIDTH), BF16),
            pltpu.SemaphoreType.DMA((2 * pixels // ROW_TILE,)),
        ],
        compiler_params=pltpu.CompilerParams(vmem_limit_bytes=2 * VMEM_BYTES),
        cost_estimate=pl.CostEstimate(flops=7 << 30, bytes_accessed=12 << 20, transcendentals=0),
        name="first_pass",
    )(ids, live, received, tile_movie, tile_foot)


def second_pass(scale, a, cross, gram, inv):
    pixels = a.shape[0]
    return pl.pallas_call(
        second_kernel,
        out_shape=(pltpu.VMEM((pixels, WIDTH), F32), pltpu.VMEM((SLOTS, BLK), F32)),
        in_specs=[VMEM_SPEC] * 5,
        out_specs=(VMEM_SPEC,) * 2,
        scratch_shapes=[pltpu.VMEM((pixels, WIDTH), BF16), pltpu.VMEM((pixels, WIDTH), BF16)],
        compiler_params=pltpu.CompilerParams(vmem_limit_bytes=VMEM_BYTES),
        cost_estimate=pl.CostEstimate(flops=4 << 30, bytes_accessed=8 << 20, transcendentals=0),
        name="second_pass",
    )(scale, a, cross, gram, inv)


def last_scaling(scale, a):
    return pl.pallas_call(
        last_kernel,
        out_shape=jax.ShapeDtypeStruct(a.shape, F32),
        in_specs=[VMEM_SPEC] * 2,
        out_specs=HBM_SPEC,
        scratch_shapes=[pltpu.VMEM(a.shape, F32), pltpu.SemaphoreType.DMA((8,))],
        compiler_params=pltpu.CompilerParams(vmem_limit_bytes=4 << 20),
        name="last_scaling",
    )(scale, a)


def totals_of(colsq, match):
    seen = to_everyone(colsq, MATES).reshape(-1, BLK)
    sums = jnp.dot(match, seen, precision=lax.Precision.HIGHEST)
    return sums[:SLOTS] + swapped(sums[SLOTS:], CORE, 1)


def per_device(movie, traces, footprints, block_ids):
    rows, cols, frames = movie.shape
    pixels = rows * cols
    n_group = lax.axis_size(PY)
    n_z = lax.axis_size("px_1")
    sizes = {axis: lax.axis_size(axis) for axis in EVERY}
    part = traces.shape[1] // n_group
    my_ids = block_ids.reshape(SLOTS)

    pieces = traces.T.reshape(n_group, 1, part, traces.shape[0])
    pieces = jnp.broadcast_to(pieces, (n_group, n_z, part, traces.shape[0]))
    pieces = pieces.reshape(n_group * n_z, part, traces.shape[0])
    pieces = pltpu.with_memory_space_constraint(pieces, pltpu.VMEM)
    spread = lax.all_to_all(pieces, COLUMN, split_axis=0, concat_axis=0, tiled=True)

    other_half = swapped(my_ids[None], "px_0", 1)
    near = jnp.concatenate([my_ids[None], other_half])
    near = jnp.concatenate([near] + [swapped(near, ("py_1", CORE), bits) for bits in (1, 2, 3)])
    plane_ids = [near] + [swapped(near, "py_0", bits) for bits in (1, 2, 3)]
    place = lax.axis_index(PLANE).reshape(1, 1)
    outgoing = select(place, plane_ids, spread)
    outgoing, plane_ids, my_ids, peer_ids = lax.optimization_barrier(
        (outgoing, plane_ids, my_ids, near[2])
    )
    every_ids = jnp.concatenate(plane_ids)
    received = lax.all_to_all(outgoing, PLANE, split_axis=0, concat_axis=0, tiled=True)
    received = received.reshape(n_group, sizes[CORE], sizes["px_0"], SLOTS, n_z, part, BLK)
    received = pltpu.with_memory_space_constraint(received, pltpu.VMEM)
    for bit in (1, 2, 4):
        far = swapped(every_ids, "px_1", bit)
        every_ids = jnp.concatenate([every_ids, far])
    mate_ids = every_ids.reshape(n_z, sizes["py_0"], sizes["py_1"], 2, sizes["px_0"], SLOTS)
    mate_ids = mate_ids[:, :, :, 0].transpose(3, 2, 0, 1, 4)
    for dim, axis in enumerate(MATES):
        mate_ids = in_place_order(mate_ids, dim, axis)
    wanted = jnp.concatenate([my_ids, peer_ids])
    match = (wanted[:, None] == mate_ids.reshape(1, -1)).astype(F32)
    live = (my_ids < NBLK).astype(F32)
    column_live = jnp.repeat(live, BLK).reshape(1, WIDTH)
    column_live, match = lax.optimization_barrier((column_live, match))

    pixall = pixels * lax.axis_size(EVERY)
    tile_movie = pltpu.with_memory_space_constraint(movie.reshape(pixels, frames), pltpu.HBM)
    tile_foot = pltpu.with_memory_space_constraint(footprints.reshape(pixels, WIDTH), pltpu.HBM)
    current, colsq, cross, gram, inv = first_pass(
        my_ids[None], column_live, received, tile_movie, tile_foot
    )
    scale = live[:, None] / jnp.sqrt(totals_of(colsq, match) / pixall + 1e-06)
    current, colsq = second_pass(scale.reshape(1, WIDTH), current, cross, gram, inv)
    scale = live[:, None] / jnp.sqrt(totals_of(colsq, match) / pixall + 1e-06)
    return last_scaling(scale.reshape(1, WIDTH), current).reshape(rows, cols, WIDTH)


def solution(mesh):
    finer = Mesh(mesh.devices.reshape(4, 2, 2, 8, 2), EVERY)
    placed = (P(PY, PX, None), P(PY, PX), P(PY, PX, None), P(PY, PX, None))

    return jax.shard_map(
        per_device, mesh=finer, in_specs=placed, out_specs=P(PY, PX, None), check_vma=False
    )
```

time: 145 us -> 145 us (level)
  other arithmetic: 3.68 us -> 1.31 us
  waiting for transfers between devices: 37.4 us -> 39.3 us
    ppermute x12, waiting for transfers between devices: 9.57 us -> 11.4 us  [swapped(): lax.ppermute(value, axis, [(i, i ^ bits) for i in range(lax.axis_size(axi...]
    mul x2 -> x0, other arithmetic: 1.64 us -> none  [per_device(): return (current * scale.reshape(1, WIDTH)).reshape(rows, cols, WIDTH)]
  transfers between devices with their start and end apart: 14 -> 14, of which waited for: 10 -> 10; matrix products, arithmetic and copies ran while one was open for 4% -> 2% of each run, Pallas kernels for 0% -> 0%
where the time goes in v3:
time: 145 us; the launch traced here: 144 us
  starting transfers between devices  46.9 us (32%)
  waiting for transfers between devices  39.3 us (27%)
  blocking collectives  37.2 us (26%)
  Pallas kernels  14.8 us (10%)
  local copies, waits for them, and re-layouts  4.2 us (3%)
    all_to_all x2, blocking collectives, to_everyone(): return lax.all_to_all(copies, axes, split_axis=0, concat_axis=0, tiled=True)  37.2 us
    all_to_all x1, waiting for transfers between devices, per_device(): lax.all_to_all(outgoing, PLANE, split_axis=0, concat_axis=0, tiled=True)  27.8 us
    ppermute x12, starting transfers between devices, swapped(): lax.ppermute(value, axis, [(i, i ^ bits) for i in range(lax.axis_size(axi...  23.7 us
    all_to_all x1, starting transfers between devices, per_device(): lax.all_to_all(pieces, COLUMN, split_axis=0, concat_axis=0, tiled=True)  13.5 us
    ppermute x12, waiting for transfers between devices, swapped(): lax.ppermute(value, axis, [(i, i ^ bits) for i in range(lax.axis_size(axi...  11.4 us
    all_to_all x1, starting transfers between devices, per_device(): lax.all_to_all(outgoing, PLANE, split_axis=0, concat_axis=0, tiled=True)  9.69 us
    pallas_call x1, Pallas kernels, first_pass(): pl.pallas_call(first_kernel, out_shape=(pltpu.VMEM((pixels, WIDTH), F32),...  8.08 us
  transfers between devices with their start and end apart: 14, of which 10 were waited for; matrix products, arithmetic and copies ran while one was open for 2% of the time, Pallas kernels for 0%

profile of v3, /device:TPU:1, one launch (start us, length us, event | category | flops | bytes accessed | tf_op | source)
XLA Modules:
  0.0 144.5 jit_solution(18330842122537503798)
XLA Ops:
  0.0 0.0 copy-start
  0.0 1.7 %broadcast_in_dim.11 = bf16[8,8,8,512]{3,2,1,0:T(8,128)(2,1)} broadcast(bf16[8,8,512]{2,1,0:T(8,128)(2,1)} %bitcast.57), dimensions={0,2,3} | broadcast | bytes 589824 | tf_op jit(solution)/shard_map/broadcast_in_dim | solution.py:277
  1.7 13.5 %all-to-all-start = ((bf16[64,8,512]{2,1,0:T(8,128)(2,1)}), bf16[64,8,512]{2,1,0:T(8,128)(2,1)S(1)}, u32[]{:S(2)}, u32[]{:S(2)}) async-start(bf16[64,8,512]{2,1,0:T(8,128)(2,1)} %bitcast.4), calls=%async_computation | async-start | bytes 1048576 | tf_op jit(solution)/shard_map/all_to_all | solution.py:280
  15.2 2.7 %collective-permute-start = (s32[1,4]{1,0:T(1,128)}, s32[1,4]{1,0:T(1,128)S(1)}, u32[]{:S(2)}, u32[]{:S(2)}) collective-permute-start(s32[1,4]{1,0:T(1,128)} %bitcast.59), channel_id=1, source_target_pairs={{0,16},{16,0},{1,17},{17,1},{2,18},{18,2},{3,19},{19,3},{4,20},{20... | collective-permute-start | bytes 56 | tf_op jit(solution)/shard_map/ppermute | solution.py:33
  17.9 1.5 %collective-permute-done = s32[1,4]{1,0:T(1,128)S(1)} collective-permute-done((s32[1,4]{1,0:T(1,128)}, s32[1,4]{1,0:T(1,128)S(1)}, u32[]{:S(2)}, u32[]{:S(2)}) %collective-permute-start) | collective-permute-done | bytes 48 | tf_op jit(solution)/shard_map/ppermute | solution.py:33
  19.4 0.7 pad_add_fusion.1
  20.0 3.2 %collective-permute-start.3 = (s32[2,4]{1,0:T(2,128)S(1)}, s32[2,4]{1,0:T(2,128)S(1)}, u32[]{:S(2)}, u32[]{:S(2)}) collective-permute-start(s32[2,4]{1,0:T(2,128)S(1)} %pad_add_fusion.1), channel_id=1, source_target_pairs={{0,33},{1,32},{32,1},{33,0},{2,35},{3,34},{34,3},{35,2},{4,37},{5,... | collective-permute-start | bytes 104 | tf_op jit(solution)/shard_map/ppermute | solution.py:33
  23.3 0.2 collective-permute-start.2
  23.4 0.3 collective-permute-start.1
  23.8 1.1 collective-permute-done.3
  24.9 1.1 collective-permute-done.2
  26.0 0.0 collective-permute-done.1
  26.0 0.7 concatenate.26.refs_0_
  26.7 2.7 %collective-permute-start.6 = (s32[8,4]{1,0:T(8,128)S(1)}, s32[8,4]{1,0:T(8,128)S(1)}, u32[]{:S(2)}, u32[]{:S(2)}) collective-permute-start(s32[8,4]{1,0:T(8,128)S(1)} %concatenate.26.refs_0_), channel_id=1, source_target_pairs={{0,192},{64,128},{128,64},{192,0},{1,193},{65,129},{129,65},{193,1... | collective-permute-start | bytes 392 | tf_op jit(solution)/shard_map/ppermute | solution.py:33
  29.4 0.4 collective-permute-start.5
  29.8 0.3 collective-permute-start.4
  30.1 0.7 collective-permute-done.6.refs_3_
  30.7 2.9 %collective-permute-done.5.refs_2_ = s32[8,4]{1,0:T(8,128)S(1)} collective-permute-done((s32[8,4]{1,0:T(8,128)S(1)}, s32[8,4]{1,0:T(8,128)S(1)}, u32[]{:S(2)}, u32[]{:S(2)}) %collective-permute-start.5) | collective-permute-done | bytes 160 | tf_op jit(solution)/shard_map/ppermute | solution.py:33
  33.7 0.0 collective-permute-done.4.refs_1_
  33.7 0.0 all-to-all-done.refs_4_
  33.7 2.5 %select.1 = bf16[32,4,8,8,128]{4,3,2,1,0:T(8,128)(2,1)} custom-call(s32[1,1]{1,0:T(1,128)} %bitcast.place_ref, s32[8,4]{1,0:T(8,128)S(1)} %concatenate.26.refs_0_, s32[8,4]{1,0:T(8,128)S(1)} %collective-permute-done.4.refs_1_, s32[8,4]{1,0:T(8,128)S(1)} %collective-permute-done.5.refs_2_, s32[8,4]{1,0:T(8,128)S(1)} %collective-permute-done.6.refs_3_, ...), custom_call_target="tpu_custom_call" | custom-call | flops 1048576 | bytes 4194304 | tf_op jit(solution)/shard_map/select/pallas_call | solution.py:76
  36.2 0.1 copy.35
  36.3 0.1 copy.36
  36.4 0.1 copy.37
  36.5 0.1 copy.38
  36.5 0.1 pad_add_fusion
  36.6 1.2 collective-permute-start.7
  37.8 1.2 collective-permute-done.7
  39.1 0.1 concatenate.29
  39.2 2.1 %collective-permute-start.8 = (s32[64,4]{0,1:T(4,128)S(1)}, s32[64,4]{0,1:T(4,128)S(1)}, u32[]{:S(2)}, u32[]{:S(2)}) collective-permute-start(s32[64,4]{0,1:T(4,128)S(1)} %concatenate.29), channel_id=1, source_target_pairs={{0,4},{2,6},{4,0},{6,2},{8,12},{10,14},{12,8},{14,10},{1,5},{3,7},... | collective-permute-start | bytes 3080 | tf_op jit(solution)/shard_map/ppermute | solution.py:33
  41.3 0.0 copy-done
  41.3 1.2 collective-permute-done.8
  42.5 0.1 concatenate.30
  42.6 4.8 %collective-permute-start.9 = (s32[128,4]{0,1:T(4,128)S(1)}, s32[128,4]{0,1:T(4,128)S(1)}, u32[]{:S(2)}, u32[]{:S(2)}) collective-permute-start(s32[128,4]{0,1:T(4,128)S(1)} %concatenate.30), channel_id=1, source_target_pairs={{0,8},{2,10},{4,12},{6,14},{8,0},{10,2},{12,4},{14,6},{1,9},{3,11}... | collective-permute-start | bytes 6152 | tf_op jit(solution)/shard_map/ppermute | solution.py:33
  47.5 0.1 pad_add_fusion.2
  47.5 9.7 %all-to-all-start.1 = ((bf16[32,4,8,8,128]{4,3,2,1,0:T(8,128)(2,1)}), bf16[32,4,8,8,128]{4,3,2,1,0:T(8,128)(2,1)S(1)}, u32[]{:S(2)}, u32[]{:S(2)}) async-start(bf16[32,4,8,8,128]{4,3,2,1,0:T(8,128)(2,1)} %select.1), calls=%async_computation.1 | async-start | bytes 4194304 | tf_op jit(solution)/shard_map/all_to_all | solution.py:292
  57.2 0.0 collective-permute-done.9
  57.3 0.1 concatenate.31
  57.4 0.1 copy.39
  57.5 0.2 reshape.90
  58.1 0.1 eq.16
  58.3 0.1 compare_convert_fusion
  58.3 0.7 div.20
  59.0 27.8 %all-to-all-done.1 = bf16[32,4,8,8,128]{4,3,2,1,0:T(8,128)(2,1)S(1)} async-done(((bf16[32,4,8,8,128]{4,3,2,1,0:T(8,128)(2,1)}), bf16[32,4,8,8,128]{4,3,2,1,0:T(8,128)(2,1)S(1)}, u32[]{:S(2)}, u32[]{:S(2)}) %all-to-all-start.1) | async-done | bytes 2097184 | tf_op jit(solution)/shard_map/all_to_all | solution.py:292
  86.8 8.1 %first_pass.1 = (f32[1024,512]{1,0:T(8,128)S(1)}, f32[4,128]{1,0:T(4,128)S(1)}, f32[1024,512]{1,0:T(8,128)S(1)}, bf16[4,512,256]{2,1,0:T(8,128)(2,1)S(1)}, f32[1,512]{1,0:T(1,128)S(1)}) custom-call(s32[1,4]{1,0:T(1,128)} %bitcast.62, f32[1,512]{1,0:T(1,128)} %bitcast.58, bf16[8,2,2,4,8,8,128]{6,5,4,3,2,1,0:T(8,128)(2,1)S(1)} %bitcast.43, ...), custom_call_target="tpu_custom_call" | custom-call | flops 7516192768 | bytes 12582912 | tf_op jit(solution)/shard_map/first_pass/pallas_call | solution.py:209
  95.0 18.5 %all_to_all.20 = f32[128,4,128]{2,1,0:T(4,128)S(1)} all-to-all(f32[128,4,128]{2,1,0:T(4,128)S(1)} %broadcast_in_dim.13), channel_id=1, replica_groups=mesh['py_0'=4,'py_1'=2,'px_0'=2,'px_1'=8,'px_2'=2] {'px_0','py_1','px_1'..., dimensions={0} | all-to-all | bytes 524288 | tf_op jit(solution)/shard_map/all_to_all | solution.py:29
  113.4 0.2 fusion
  113.7 3.1 %collective-permute-start.10 = (f32[4,128]{1,0:T(4,128)S(1)}, f32[4,128]{1,0:T(4,128)S(1)}, u32[]{:S(2)}, u32[]{:S(2)}) collective-permute-start(f32[4,128]{1,0:T(4,128)S(1)} %slice.21), channel_id=1, source_target_pairs={{0,1},{1,0},{2,3},{3,2},{4,5},{5,4},{6,7},{7,6},{8,9},{9,8},{10,11... | collective-permute-start | bytes 6152 | tf_op jit(solution)/shard_map/ppermute | solution.py:33
  116.7 0.8 collective-permute-done.10
  117.6 0.1 rsqrt_multiply_fusion.1
  117.6 2.7 %second_pass.1 = (f32[1024,512]{1,0:T(8,128)S(1)}, f32[4,128]{1,0:T(4,128)S(1)}) custom-call(f32[1,512]{1,0:T(1,128)S(1)} %bitcast.45, f32[1024,512]{1,0:T(8,128)S(1)} %get-tuple-element.31.old_ref, f32[1024,512]{1,0:T(8,128)S(1)} %get-tuple-element.32.cross_ref, bf16[4,512,256]{2,1,0:T(8,128)(2,1)S(1)} %get-tuple-element.33.gram_ref, ...), custom_call_target="tpu_custom_call" | custom-call | flops 4294967296 | bytes 8388608 | tf_op jit(solution)/shard_map/second_pass/pallas_call | solution.py:237
  120.4 18.7 %all_to_all.21 = f32[128,4,128]{2,1,0:T(4,128)S(1)} all-to-all(f32[128,4,128]{2,1,0:T(4,128)S(1)} %broadcast_in_dim.14), channel_id=1, replica_groups=mesh['py_0'=4,'py_1'=2,'px_0'=2,'px_1'=8,'px_2'=2] {'px_0','py_1','px_1'..., dimensions={0} | all-to-all | bytes 524288 | tf_op jit(solution)/shard_map/all_to_all | solution.py:29
  139.1 0.2 fusion.1
  139.4 2.7 %collective-permute-start.11 = (f32[4,128]{1,0:T(4,128)S(1)}, f32[4,128]{1,0:T(4,128)S(1)}, u32[]{:S(2)}, u32[]{:S(2)}) collective-permute-start(f32[4,128]{1,0:T(4,128)S(1)} %slice.23), channel_id=1, source_target_pairs={{0,1},{1,0},{2,3},{3,2},{4,5},{5,4},{6,7},{7,6},{8,9},{9,8},{10,11... | collective-permute-start | bytes 6152 | tf_op jit(solution)/shard_map/ppermute | solution.py:33
  142.0 0.8 collective-permute-done.11
  142.9 0.1 rsqrt_multiply_fusion
  142.9 1.4 last_scaling.1
  (20 shorter events, 0.5 us)
Async XLA Ops:
  0.0 41.3 %copy-start = (s32[1,1,4]{2,1,0:T(1,128)S(1)}, s32[1,1,4]{2,1,0:T(1,128)}, u32[]{:S(2)}) copy-start(s32[1,1,4]{2,1,0:T(1,128)} %param.7) | copy-start | bytes 52
  1.7 32.0 %all-to-all-start = ((bf16[64,8,512]{2,1,0:T(8,128)(2,1)}), bf16[64,8,512]{2,1,0:T(8,128)(2,1)S(1)}, u32[]{:S(2)}, u32[]{:S(2)}) async-start(bf16[64,8,512]{2,1,0:T(8,128)(2,1)} %bitcast.4), calls=%async_computation | async-start | bytes 1048576 | tf_op jit(solution)/shard_map/all_to_all | solution.py:280
  15.2 4.2 %collective-permute-start = (s32[1,4]{1,0:T(1,128)}, s32[1,4]{1,0:T(1,128)S(1)}, u32[]{:S(2)}, u32[]{:S(2)}) collective-permute-start(s32[1,4]{1,0:T(1,128)} %bitcast.59), channel_id=1, source_target_pairs={{0,16},{16,0},{1,17},{17,1},{2,18},{18,2},{3,19},{19,3},{4,20},{20... | collective-permute-start | bytes 56 | tf_op jit(solution)/shard_map/ppermute | solution.py:33
  20.0 4.8 %collective-permute-start.3 = (s32[2,4]{1,0:T(2,128)S(1)}, s32[2,4]{1,0:T(2,128)S(1)}, u32[]{:S(2)}, u32[]{:S(2)}) collective-permute-start(s32[2,4]{1,0:T(2,128)S(1)} %pad_add_fusion.1), channel_id=1, source_target_pairs={{0,33},{1,32},{32,1},{33,0},{2,35},{3,34},{34,3},{35,2},{4,37},{5,... | collective-permute-start | bytes 104 | tf_op jit(solution)/shard_map/ppermute | solution.py:33
  23.3 2.7 %collective-permute-start.2 = (s32[2,4]{1,0:T(2,128)S(1)}, s32[2,4]{1,0:T(2,128)S(1)}, u32[]{:S(2)}, u32[]{:S(2)}) collective-permute-start(s32[2,4]{1,0:T(2,128)S(1)} %pad_add_fusion.1), channel_id=1, source_target_pairs={{0,32},{1,33},{32,0},{33,1},{2,34},{3,35},{34,2},{35,3},{4,36},{5,... | collective-permute-start | bytes 104 | tf_op jit(solution)/shard_map/ppermute | solution.py:33
  23.4 2.6 %collective-permute-start.1 = (s32[2,4]{1,0:T(2,128)S(1)}, s32[2,4]{1,0:T(2,128)S(1)}, u32[]{:S(2)}, u32[]{:S(2)}) collective-permute-start(s32[2,4]{1,0:T(2,128)S(1)} %pad_add_fusion.1), channel_id=1, source_target_pairs={{0,1},{1,0},{32,33},{33,32},{2,3},{3,2},{34,35},{35,34},{4,5},{5,4... | collective-permute-start | bytes 104 | tf_op jit(solution)/shard_map/ppermute | solution.py:33
  26.7 4.1 %collective-permute-start.6 = (s32[8,4]{1,0:T(8,128)S(1)}, s32[8,4]{1,0:T(8,128)S(1)}, u32[]{:S(2)}, u32[]{:S(2)}) collective-permute-start(s32[8,4]{1,0:T(8,128)S(1)} %concatenate.26.refs_0_), channel_id=1, source_target_pairs={{0,192},{64,128},{128,64},{192,0},{1,193},{65,129},{129,65},{193,1... | collective-permute-start | bytes 392 | tf_op jit(solution)/shard_map/ppermute | solution.py:33
  29.4 4.3 %collective-permute-start.5 = (s32[8,4]{1,0:T(8,128)S(1)}, s32[8,4]{1,0:T(8,128)S(1)}, u32[]{:S(2)}, u32[]{:S(2)}) collective-permute-start(s32[8,4]{1,0:T(8,128)S(1)} %concatenate.26.refs_0_), channel_id=1, source_target_pairs={{0,128},{64,192},{128,0},{192,64},{1,129},{65,193},{129,1},{193,65... | collective-permute-start | bytes 392 | tf_op jit(solution)/shard_map/ppermute | solution.py:33
  29.8 3.9 %collective-permute-start.4 = (s32[8,4]{1,0:T(8,128)S(1)}, s32[8,4]{1,0:T(8,128)S(1)}, u32[]{:S(2)}, u32[]{:S(2)}) collective-permute-start(s32[8,4]{1,0:T(8,128)S(1)} %concatenate.26.refs_0_), channel_id=1, source_target_pairs={{0,64},{64,0},{128,192},{192,128},{1,65},{65,1},{129,193},{193,129... | collective-permute-start | bytes 392 | tf_op jit(solution)/shard_map/ppermute | solution.py:33
  36.6 2.5 %collective-permute-start.7 = (s32[32,4]{0,1:T(4,128)S(1)}, s32[32,4]{0,1:T(4,128)S(1)}, u32[]{:S(2)}, u32[]{:S(2)}) collective-permute-start(s32[32,4]{0,1:T(4,128)S(1)} %pad_add_fusion), channel_id=1, source_target_pairs={{0,2},{2,0},{4,6},{6,4},{8,10},{10,8},{12,14},{14,12},{1,3},{3,1},... | collective-permute-start | bytes 1544 | tf_op jit(solution)/shard_map/ppermute | solution.py:33
  39.2 3.3 %collective-permute-start.8 = (s32[64,4]{0,1:T(4,128)S(1)}, s32[64,4]{0,1:T(4,128)S(1)}, u32[]{:S(2)}, u32[]{:S(2)}) collective-permute-start(s32[64,4]{0,1:T(4,128)S(1)} %concatenate.29), channel_id=1, source_target_pairs={{0,4},{2,6},{4,0},{6,2},{8,12},{10,14},{12,8},{14,10},{1,5},{3,7},... | collective-permute-start | bytes 3080 | tf_op jit(solution)/shard_map/ppermute | solution.py:33
  42.6 14.6 %collective-permute-start.9 = (s32[128,4]{0,1:T(4,128)S(1)}, s32[128,4]{0,1:T(4,128)S(1)}, u32[]{:S(2)}, u32[]{:S(2)}) collective-permute-start(s32[128,4]{0,1:T(4,128)S(1)} %concatenate.30), channel_id=1, source_target_pairs={{0,8},{2,10},{4,12},{6,14},{8,0},{10,2},{12,4},{14,6},{1,9},{3,11}... | collective-permute-start | bytes 6152 | tf_op jit(solution)/shard_map/ppermute | solution.py:33
  47.5 39.3 %all-to-all-start.1 = ((bf16[32,4,8,8,128]{4,3,2,1,0:T(8,128)(2,1)}), bf16[32,4,8,8,128]{4,3,2,1,0:T(8,128)(2,1)S(1)}, u32[]{:S(2)}, u32[]{:S(2)}) async-start(bf16[32,4,8,8,128]{4,3,2,1,0:T(8,128)(2,1)} %select.1), calls=%async_computation.1 | async-start | bytes 4194304 | tf_op jit(solution)/shard_map/all_to_all | solution.py:292
  113.7 3.9 %collective-permute-start.10 = (f32[4,128]{1,0:T(4,128)S(1)}, f32[4,128]{1,0:T(4,128)S(1)}, u32[]{:S(2)}, u32[]{:S(2)}) collective-permute-start(f32[4,128]{1,0:T(4,128)S(1)} %slice.21), channel_id=1, source_target_pairs={{0,1},{1,0},{2,3},{3,2},{4,5},{5,4},{6,7},{7,6},{8,9},{9,8},{10,11... | collective-permute-start | bytes 6152 | tf_op jit(solution)/shard_map/ppermute | solution.py:33
  139.4 3.5 %collective-permute-start.11 = (f32[4,128]{1,0:T(4,128)S(1)}, f32[4,128]{1,0:T(4,128)S(1)}, u32[]{:S(2)}, u32[]{:S(2)}) collective-permute-start(f32[4,128]{1,0:T(4,128)S(1)} %slice.23), channel_id=1, source_target_pairs={{0,1},{1,0},{2,3},{3,2},{4,5},{5,4},{6,7},{7,6},{8,9},{9,8},{10,11... | collective-permute-start | bytes 6152 | tf_op jit(solution)/shard_map/ppermute | solution.py:33

commit v4 on v3

--- a/solution.py
+++ b/solution.py
@@ -45,18 +45,43 @@
     return value
 
 
-def select_kernel(place_ref, *refs):
-    *ids_refs, rows_ref, out_hbm, sem = refs
-    place = place_ref[0, 0]
-    chunk = ids_refs[0].shape[0]
+def stage_kernel(place_ref, *refs):
+    *ids_refs, out_ref, sem = refs
+    copies = [pltpu.make_async_copy(ids_ref, out_ref.at[i], sem) for i, ids_ref in enumerate(ids_refs)]
+    out_ref[len(ids_refs), 0, 0] = place_ref[0, 0]
+    for copy in copies:
+        copy.start()
+    for copy in copies:
+        copy.wait()
+
+
+def stage(place, ids_pieces):
+    vmem = pl.BlockSpec(memory_space=pltpu.VMEM)
+    smem = pl.BlockSpec(memory_space=pltpu.SMEM)
+    n = len(ids_pieces)
+    return pl.pallas_call(
+        stage_kernel,
+        out_shape=pltpu.SMEM((n + 1, *ids_pieces[0].shape), jnp.int32),
+        in_specs=[smem] + [vmem] * n,
+        out_specs=smem,
+        scratch_shapes=[pltpu.SemaphoreType.DMA],
+        compiler_params=pltpu.CompilerParams(vmem_limit_bytes=2 << 20),
+        name="stage",
+    )(place, *ids_pieces)
+
+
+def select_kernel(ids_ref, rows_ref, out_hbm, sem):
+    pieces, chunk, _ = ids_ref.shape
+    pieces -= 1
+    place = ids_ref[pieces, 0, 0]
     depth = rows_ref.shape[0] // (NBLK // SLOTS)
-    for far, ids_ref in enumerate(ids_refs):
+    for far in range(pieces):
 
         @pl.loop(0, chunk, unroll=True)
         def _(near):
             tile = (far * chunk + near) ^ place
             for slot in range(SLOTS):
-                block = jnp.minimum(ids_ref[near, slot], NBLK - 1)
+                block = jnp.minimum(ids_ref[far, near, slot], NBLK - 1)
                 group = pl.multiple_of((block // SLOTS) * depth, depth)
                 lane = pl.multiple_of((block % SLOTS) * BLK, BLK)
                 pltpu.make_async_copy(
@@ -68,23 +93,19 @@
     pltpu.make_async_copy(out_hbm, out_hbm, sem).wait()
 
 
-def select(place, ids_pieces, rows):
+def select(staged, rows):
     depth = rows.shape[0] // (NBLK // SLOTS)
-    tiles = sum(piece.shape[0] for piece in ids_pieces)
-    smem = pl.BlockSpec(memory_space=pltpu.SMEM)
-    anywhere = pl.BlockSpec(memory_space=pltpu.HBM)
+    tiles = (staged.shape[0] - 1) * staged.shape[1]
     return pl.pallas_call(
         select_kernel,
         out_shape=jax.ShapeDtypeStruct((tiles, SLOTS, depth, rows.shape[1], BLK), rows.dtype),
-        in_specs=[smem] * (1 + len(ids_pieces)) + [pl.BlockSpec(memory_space=pltpu.VMEM)],
-        out_specs=anywhere,
-        scratch_shapes=[
-            pltpu.SemaphoreType.DMA,
-        ],
+        in_specs=[pl.BlockSpec(memory_space=pltpu.SMEM), pl.BlockSpec(memory_space=pltpu.VMEM)],
+        out_specs=pl.BlockSpec(memory_space=pltpu.HBM),
+        scratch_shapes=[pltpu.SemaphoreType.DMA],
+        compiler_params=pltpu.CompilerParams(vmem_limit_bytes=2 << 20),
         cost_estimate=pl.CostEstimate(flops=1 << 20, bytes_accessed=1 << 22, transcendentals=0),
-        compiler_params=pltpu.CompilerParams(vmem_limit_bytes=2 << 20),
         name="select",
-    )(place, *ids_pieces, rows)
+    )(staged, rows)
 
 
 def sweep(base, a_ref, hi_ref, lo_ref, cross_ref, gram_ref, inv_ref, colsq_ref):
@@ -284,7 +305,7 @@
     near = jnp.concatenate([near] + [swapped(near, ("py_1", CORE), bits) for bits in (1, 2, 3)])
     plane_ids = [near] + [swapped(near, "py_0", bits) for bits in (1, 2, 3)]
     place = lax.axis_index(PLANE).reshape(1, 1)
-    outgoing = select(place, plane_ids, spread)
+    outgoing = select(stage(place, plane_ids), spread)
     outgoing, plane_ids, my_ids, peer_ids = lax.optimization_barrier(
         (outgoing, plane_ids, my_ids, near[2])
     )

time: 145 us -> 145 us (level)
  transfers between devices with their start and end apart: 14 -> 14, of which waited for: 10 -> 10; matrix products, arithmetic and copies ran while one was open for 2% -> 2% of each run, Pallas kernels for 0% -> 1%
where the time goes in v4:
time: 145 us
  starting transfers between devices  46.9 us (32%)
  waiting for transfers between devices  39.3 us (27%)
  blocking collectives  37.2 us (26%)
  Pallas kernels  14.8 us (10%)
  local copies, waits for them, and re-layouts  4.2 us (3%)
    all_to_all x2, blocking collectives, to_everyone(): return lax.all_to_all(copies, axes, split_axis=0, concat_axis=0, tiled=True)  37.2 us
    all_to_all x1, waiting for transfers between devices, per_device(): lax.all_to_all(outgoing, PLANE, split_axis=0, concat_axis=0, tiled=True)  27.8 us
    ppermute x12, starting transfers between devices, swapped(): lax.ppermute(value, axis, [(i, i ^ bits) for i in range(lax.axis_size(axi...  23.7 us
    all_to_all x1, starting transfers between devices, per_device(): lax.all_to_all(pieces, COLUMN, split_axis=0, concat_axis=0, tiled=True)  13.5 us
    ppermute x12, waiting for transfers between devices, swapped(): lax.ppermute(value, axis, [(i, i ^ bits) for i in range(lax.axis_size(axi...  11.4 us
    all_to_all x1, starting transfers between devices, per_device(): lax.all_to_all(outgoing, PLANE, split_axis=0, concat_axis=0, tiled=True)  9.69 us
    pallas_call x1, Pallas kernels, first_pass(): pl.pallas_call(first_kernel, out_shape=(pltpu.VMEM((pixels, WIDTH), F32),...  8.08 us
  transfers between devices with their start and end apart: 14, of which 10 were waited for; matrix products, arithmetic and copies ran while one was open for 2% of the time, Pallas kernels for 1%

profile of v4, /device:TPU:1, one launch (start us, length us, event | category | flops | bytes accessed | tf_op | source)
XLA Modules:
  0.0 144.5 jit_solution(2053459550619419808)
XLA Ops:
  0.0 0.0 copy-start
  0.0 1.7 %broadcast_in_dim.11 = bf16[8,8,8,512]{3,2,1,0:T(8,128)(2,1)} broadcast(bf16[8,8,512]{2,1,0:T(8,128)(2,1)} %bitcast.57), dimensions={0,2,3} | broadcast | bytes 589824 | tf_op jit(solution)/shard_map/broadcast_in_dim | solution.py:298
  1.7 13.5 %all-to-all-start = ((bf16[64,8,512]{2,1,0:T(8,128)(2,1)}), bf16[64,8,512]{2,1,0:T(8,128)(2,1)S(1)}, u32[]{:S(2)}, u32[]{:S(2)}) async-start(bf16[64,8,512]{2,1,0:T(8,128)(2,1)} %bitcast.4), calls=%async_computation | async-start | bytes 1048576 | tf_op jit(solution)/shard_map/all_to_all | solution.py:301
  15.2 2.7 %collective-permute-start = (s32[1,4]{1,0:T(1,128)}, s32[1,4]{1,0:T(1,128)S(1)}, u32[]{:S(2)}, u32[]{:S(2)}) collective-permute-start(s32[1,4]{1,0:T(1,128)} %bitcast.59), channel_id=1, source_target_pairs={{0,16},{16,0},{1,17},{17,1},{2,18},{18,2},{3,19},{19,3},{4,20},{20... | collective-permute-start | bytes 56 | tf_op jit(solution)/shard_map/ppermute | solution.py:33
  17.9 1.5 %collective-permute-done = s32[1,4]{1,0:T(1,128)S(1)} collective-permute-done((s32[1,4]{1,0:T(1,128)}, s32[1,4]{1,0:T(1,128)S(1)}, u32[]{:S(2)}, u32[]{:S(2)}) %collective-permute-start) | collective-permute-done | bytes 48 | tf_op jit(solution)/shard_map/ppermute | solution.py:33
  19.4 0.7 pad_add_fusion.1
  20.0 3.2 %collective-permute-start.3 = (s32[2,4]{1,0:T(2,128)S(1)}, s32[2,4]{1,0:T(2,128)S(1)}, u32[]{:S(2)}, u32[]{:S(2)}) collective-permute-start(s32[2,4]{1,0:T(2,128)S(1)} %pad_add_fusion.1), channel_id=1, source_target_pairs={{0,33},{1,32},{32,1},{33,0},{2,35},{3,34},{34,3},{35,2},{4,37},{5,... | collective-permute-start | bytes 104 | tf_op jit(solution)/shard_map/ppermute | solution.py:33
  23.3 0.2 collective-permute-start.2
  23.4 0.3 collective-permute-start.1
  23.8 1.1 collective-permute-done.3
  24.9 1.1 collective-permute-done.2
  26.0 0.0 collective-permute-done.1
  26.0 0.7 concatenate.26.refs_0_
  26.7 2.7 %collective-permute-start.6 = (s32[8,4]{1,0:T(8,128)S(1)}, s32[8,4]{1,0:T(8,128)S(1)}, u32[]{:S(2)}, u32[]{:S(2)}) collective-permute-start(s32[8,4]{1,0:T(8,128)S(1)} %concatenate.26.refs_0_), channel_id=1, source_target_pairs={{0,192},{64,128},{128,64},{192,0},{1,193},{65,129},{129,65},{193,1... | collective-permute-start | bytes 392 | tf_op jit(solution)/shard_map/ppermute | solution.py:33
  29.4 0.4 collective-permute-start.5
  29.8 0.3 collective-permute-start.4
  30.1 0.7 collective-permute-done.6.refs_3_
  30.7 2.9 %collective-permute-done.5.refs_2_ = s32[8,4]{1,0:T(8,128)S(1)} collective-permute-done((s32[8,4]{1,0:T(8,128)S(1)}, s32[8,4]{1,0:T(8,128)S(1)}, u32[]{:S(2)}, u32[]{:S(2)}) %collective-permute-start.5) | collective-permute-done | bytes 160 | tf_op jit(solution)/shard_map/ppermute | solution.py:33
  33.7 0.0 collective-permute-done.4.refs_1_
  33.7 0.8 stage.1.ids_ref
  34.5 0.0 all-to-all-done.rows_ref
  34.5 1.8 %select.1 = bf16[32,4,8,8,128]{4,3,2,1,0:T(8,128)(2,1)} custom-call(s32[5,8,4]{2,1,0:T(8,128)S(4)} %stage.1.ids_ref, bf16[64,8,512]{2,1,0:T(8,128)(2,1)S(1)} %all-to-all-done.rows_ref), custom_call_target="tpu_custom_call" | custom-call | flops 1048576 | bytes 4194304 | tf_op jit(solution)/shard_map/select/pallas_call | solution.py:99
  36.3 0.1 copy.35
  36.4 0.1 copy.36
  36.4 0.1 copy.37
  36.5 0.1 copy.38
  36.6 0.1 pad_add_fusion
  36.7 1.2 collective-permute-start.7
  37.9 1.2 collective-permute-done.7
  39.1 0.1 concatenate.29
  39.2 2.1 %collective-permute-start.8 = (s32[64,4]{0,1:T(4,128)S(1)}, s32[64,4]{0,1:T(4,128)S(1)}, u32[]{:S(2)}, u32[]{:S(2)}) collective-permute-start(s32[64,4]{0,1:T(4,128)S(1)} %concatenate.29), channel_id=1, source_target_pairs={{0,4},{2,6},{4,0},{6,2},{8,12},{10,14},{12,8},{14,10},{1,5},{3,7},... | collective-permute-start | bytes 3080 | tf_op jit(solution)/shard_map/ppermute | solution.py:33
  41.3 0.0 copy-done
  41.3 1.2 collective-permute-done.8
  42.6 0.1 concatenate.30
  42.7 4.8 %collective-permute-start.9 = (s32[128,4]{0,1:T(4,128)S(1)}, s32[128,4]{0,1:T(4,128)S(1)}, u32[]{:S(2)}, u32[]{:S(2)}) collective-permute-start(s32[128,4]{0,1:T(4,128)S(1)} %concatenate.30), channel_id=1, source_target_pairs={{0,8},{2,10},{4,12},{6,14},{8,0},{10,2},{12,4},{14,6},{1,9},{3,11}... | collective-permute-start | bytes 6152 | tf_op jit(solution)/shard_map/ppermute | solution.py:33
  47.5 0.1 pad_add_fusion.2
  47.6 9.7 %all-to-all-start.1 = ((bf16[32,4,8,8,128]{4,3,2,1,0:T(8,128)(2,1)}), bf16[32,4,8,8,128]{4,3,2,1,0:T(8,128)(2,1)S(1)}, u32[]{:S(2)}, u32[]{:S(2)}) async-start(bf16[32,4,8,8,128]{4,3,2,1,0:T(8,128)(2,1)} %select.1), calls=%async_computation.1 | async-start | bytes 4194304 | tf_op jit(solution)/shard_map/all_to_all | solution.py:313
  57.3 0.0 collective-permute-done.9
  57.3 0.1 concatenate.31
  57.4 0.1 copy.39
  57.6 0.2 reshape.90
  58.2 0.1 eq.16
  58.3 0.1 compare_convert_fusion
  58.4 0.7 div.20
  59.0 27.8 %all-to-all-done.1 = bf16[32,4,8,8,128]{4,3,2,1,0:T(8,128)(2,1)S(1)} async-done(((bf16[32,4,8,8,128]{4,3,2,1,0:T(8,128)(2,1)}), bf16[32,4,8,8,128]{4,3,2,1,0:T(8,128)(2,1)S(1)}, u32[]{:S(2)}, u32[]{:S(2)}) %all-to-all-start.1) | async-done | bytes 2097184 | tf_op jit(solution)/shard_map/all_to_all | solution.py:313
  86.9 8.1 %first_pass.1 = (f32[1024,512]{1,0:T(8,128)S(1)}, f32[4,128]{1,0:T(4,128)S(1)}, f32[1024,512]{1,0:T(8,128)S(1)}, bf16[4,512,256]{2,1,0:T(8,128)(2,1)S(1)}, f32[1,512]{1,0:T(1,128)S(1)}) custom-call(s32[1,4]{1,0:T(1,128)} %bitcast.62, f32[1,512]{1,0:T(1,128)} %bitcast.58, bf16[8,2,2,4,8,8,128]{6,5,4,3,2,1,0:T(8,128)(2,1)S(1)} %bitcast.43, ...), custom_call_target="tpu_custom_call" | custom-call | flops 7516192768 | bytes 12582912 | tf_op jit(solution)/shard_map/first_pass/pallas_call | solution.py:230
  95.0 18.5 %all_to_all.20 = f32[128,4,128]{2,1,0:T(4,128)S(1)} all-to-all(f32[128,4,128]{2,1,0:T(4,128)S(1)} %broadcast_in_dim.13), channel_id=1, replica_groups=mesh['py_0'=4,'py_1'=2,'px_0'=2,'px_1'=8,'px_2'=2] {'px_0','py_1','px_1'..., dimensions={0} | all-to-all | bytes 524288 | tf_op jit(solution)/shard_map/all_to_all | solution.py:29
  113.5 0.2 fusion
  113.7 3.0 %collective-permute-start.10 = (f32[4,128]{1,0:T(4,128)S(1)}, f32[4,128]{1,0:T(4,128)S(1)}, u32[]{:S(2)}, u32[]{:S(2)}) collective-permute-start(f32[4,128]{1,0:T(4,128)S(1)} %slice.21), channel_id=1, source_target_pairs={{0,1},{1,0},{2,3},{3,2},{4,5},{5,4},{6,7},{7,6},{8,9},{9,8},{10,11... | collective-permute-start | bytes 6152 | tf_op jit(solution)/shard_map/ppermute | solution.py:33
  116.8 0.8 collective-permute-done.10
  117.6 0.1 rsqrt_multiply_fusion.1
  117.7 2.7 %second_pass.1 = (f32[1024,512]{1,0:T(8,128)S(1)}, f32[4,128]{1,0:T(4,128)S(1)}) custom-call(f32[1,512]{1,0:T(1,128)S(1)} %bitcast.45, f32[1024,512]{1,0:T(8,128)S(1)} %get-tuple-element.31.old_ref, f32[1024,512]{1,0:T(8,128)S(1)} %get-tuple-element.32.cross_ref, bf16[4,512,256]{2,1,0:T(8,128)(2,1)S(1)} %get-tuple-element.33.gram_ref, ...), custom_call_target="tpu_custom_call" | custom-call | flops 4294967296 | bytes 8388608 | tf_op jit(solution)/shard_map/second_pass/pallas_call | solution.py:258
  120.5 18.7 %all_to_all.21 = f32[128,4,128]{2,1,0:T(4,128)S(1)} all-to-all(f32[128,4,128]{2,1,0:T(4,128)S(1)} %broadcast_in_dim.14), channel_id=1, replica_groups=mesh['py_0'=4,'py_1'=2,'px_0'=2,'px_1'=8,'px_2'=2] {'px_0','py_1','px_1'..., dimensions={0} | all-to-all | bytes 524288 | tf_op jit(solution)/shard_map/all_to_all | solution.py:29
  139.2 0.2 fusion.1
  139.4 2.7 %collective-permute-start.11 = (f32[4,128]{1,0:T(4,128)S(1)}, f32[4,128]{1,0:T(4,128)S(1)}, u32[]{:S(2)}, u32[]{:S(2)}) collective-permute-start(f32[4,128]{1,0:T(4,128)S(1)} %slice.23), channel_id=1, source_target_pairs={{0,1},{1,0},{2,3},{3,2},{4,5},{5,4},{6,7},{7,6},{8,9},{9,8},{10,11... | collective-permute-start | bytes 6152 | tf_op jit(solution)/shard_map/ppermute | solution.py:33
  142.1 0.8 collective-permute-done.11
  142.9 0.1 rsqrt_multiply_fusion
  143.0 1.4 last_scaling.1
  (20 shorter events, 0.5 us)
Async XLA Ops:
  0.0 41.3 %copy-start = (s32[1,1,4]{2,1,0:T(1,128)S(1)}, s32[1,1,4]{2,1,0:T(1,128)}, u32[]{:S(2)}) copy-start(s32[1,1,4]{2,1,0:T(1,128)} %param.7) | copy-start | bytes 52
  1.7 32.8 %all-to-all-start = ((bf16[64,8,512]{2,1,0:T(8,128)(2,1)}), bf16[64,8,512]{2,1,0:T(8,128)(2,1)S(1)}, u32[]{:S(2)}, u32[]{:S(2)}) async-start(bf16[64,8,512]{2,1,0:T(8,128)(2,1)} %bitcast.4), calls=%async_computation | async-start | bytes 1048576 | tf_op jit(solution)/shard_map/all_to_all | solution.py:301
  15.2 4.2 %collective-permute-start = (s32[1,4]{1,0:T(1,128)}, s32[1,4]{1,0:T(1,128)S(1)}, u32[]{:S(2)}, u32[]{:S(2)}) collective-permute-start(s32[1,4]{1,0:T(1,128)} %bitcast.59), channel_id=1, source_target_pairs={{0,16},{16,0},{1,17},{17,1},{2,18},{18,2},{3,19},{19,3},{4,20},{20... | collective-permute-start | bytes 56 | tf_op jit(solution)/shard_map/ppermute | solution.py:33
  20.0 4.8 %collective-permute-start.3 = (s32[2,4]{1,0:T(2,128)S(1)}, s32[2,4]{1,0:T(2,128)S(1)}, u32[]{:S(2)}, u32[]{:S(2)}) collective-permute-start(s32[2,4]{1,0:T(2,128)S(1)} %pad_add_fusion.1), channel_id=1, source_target_pairs={{0,33},{1,32},{32,1},{33,0},{2,35},{3,34},{34,3},{35,2},{4,37},{5,... | collective-permute-start | bytes 104 | tf_op jit(solution)/shard_map/ppermute | solution.py:33
  23.3 2.7 %collective-permute-start.2 = (s32[2,4]{1,0:T(2,128)S(1)}, s32[2,4]{1,0:T(2,128)S(1)}, u32[]{:S(2)}, u32[]{:S(2)}) collective-permute-start(s32[2,4]{1,0:T(2,128)S(1)} %pad_add_fusion.1), channel_id=1, source_target_pairs={{0,32},{1,33},{32,0},{33,1},{2,34},{3,35},{34,2},{35,3},{4,36},{5,... | collective-permute-start | bytes 104 | tf_op jit(solution)/shard_map/ppermute | solution.py:33
  23.4 2.6 %collective-permute-start.1 = (s32[2,4]{1,0:T(2,128)S(1)}, s32[2,4]{1,0:T(2,128)S(1)}, u32[]{:S(2)}, u32[]{:S(2)}) collective-permute-start(s32[2,4]{1,0:T(2,128)S(1)} %pad_add_fusion.1), channel_id=1, source_target_pairs={{0,1},{1,0},{32,33},{33,32},{2,3},{3,2},{34,35},{35,34},{4,5},{5,4... | collective-permute-start | bytes 104 | tf_op jit(solution)/shard_map/ppermute | solution.py:33
  26.7 4.1 %collective-permute-start.6 = (s32[8,4]{1,0:T(8,128)S(1)}, s32[8,4]{1,0:T(8,128)S(1)}, u32[]{:S(2)}, u32[]{:S(2)}) collective-permute-start(s32[8,4]{1,0:T(8,128)S(1)} %concatenate.26.refs_0_), channel_id=1, source_target_pairs={{0,192},{64,128},{128,64},{192,0},{1,193},{65,129},{129,65},{193,1... | collective-permute-start | bytes 392 | tf_op jit(solution)/shard_map/ppermute | solution.py:33
  29.4 4.3 %collective-permute-start.5 = (s32[8,4]{1,0:T(8,128)S(1)}, s32[8,4]{1,0:T(8,128)S(1)}, u32[]{:S(2)}, u32[]{:S(2)}) collective-permute-start(s32[8,4]{1,0:T(8,128)S(1)} %concatenate.26.refs_0_), channel_id=1, source_target_pairs={{0,128},{64,192},{128,0},{192,64},{1,129},{65,193},{129,1},{193,65... | collective-permute-start | bytes 392 | tf_op jit(solution)/shard_map/ppermute | solution.py:33
  29.8 3.9 %collective-permute-start.4 = (s32[8,4]{1,0:T(8,128)S(1)}, s32[8,4]{1,0:T(8,128)S(1)}, u32[]{:S(2)}, u32[]{:S(2)}) collective-permute-start(s32[8,4]{1,0:T(8,128)S(1)} %concatenate.26.refs_0_), channel_id=1, source_target_pairs={{0,64},{64,0},{128,192},{192,128},{1,65},{65,1},{129,193},{193,129... | collective-permute-start | bytes 392 | tf_op jit(solution)/shard_map/ppermute | solution.py:33
  36.7 2.5 %collective-permute-start.7 = (s32[32,4]{0,1:T(4,128)S(1)}, s32[32,4]{0,1:T(4,128)S(1)}, u32[]{:S(2)}, u32[]{:S(2)}) collective-permute-start(s32[32,4]{0,1:T(4,128)S(1)} %pad_add_fusion), channel_id=1, source_target_pairs={{0,2},{2,0},{4,6},{6,4},{8,10},{10,8},{12,14},{14,12},{1,3},{3,1},... | collective-permute-start | bytes 1544 | tf_op jit(solution)/shard_map/ppermute | solution.py:33
  39.2 3.3 %collective-permute-start.8 = (s32[64,4]{0,1:T(4,128)S(1)}, s32[64,4]{0,1:T(4,128)S(1)}, u32[]{:S(2)}, u32[]{:S(2)}) collective-permute-start(s32[64,4]{0,1:T(4,128)S(1)} %concatenate.29), channel_id=1, source_target_pairs={{0,4},{2,6},{4,0},{6,2},{8,12},{10,14},{12,8},{14,10},{1,5},{3,7},... | collective-permute-start | bytes 3080 | tf_op jit(solution)/shard_map/ppermute | solution.py:33
  42.7 14.6 %collective-permute-start.9 = (s32[128,4]{0,1:T(4,128)S(1)}, s32[128,4]{0,1:T(4,128)S(1)}, u32[]{:S(2)}, u32[]{:S(2)}) collective-permute-start(s32[128,4]{0,1:T(4,128)S(1)} %concatenate.30), channel_id=1, source_target_pairs={{0,8},{2,10},{4,12},{6,14},{8,0},{10,2},{12,4},{14,6},{1,9},{3,11}... | collective-permute-start | bytes 6152 | tf_op jit(solution)/shard_map/ppermute | solution.py:33
  47.6 39.3 %all-to-all-start.1 = ((bf16[32,4,8,8,128]{4,3,2,1,0:T(8,128)(2,1)}), bf16[32,4,8,8,128]{4,3,2,1,0:T(8,128)(2,1)S(1)}, u32[]{:S(2)}, u32[]{:S(2)}) async-start(bf16[32,4,8,8,128]{4,3,2,1,0:T(8,128)(2,1)} %select.1), calls=%async_computation.1 | async-start | bytes 4194304 | tf_op jit(solution)/shard_map/all_to_all | solution.py:313
  113.7 3.9 %collective-permute-start.10 = (f32[4,128]{1,0:T(4,128)S(1)}, f32[4,128]{1,0:T(4,128)S(1)}, u32[]{:S(2)}, u32[]{:S(2)}) collective-permute-start(f32[4,128]{1,0:T(4,128)S(1)} %slice.21), channel_id=1, source_target_pairs={{0,1},{1,0},{2,3},{3,2},{4,5},{5,4},{6,7},{7,6},{8,9},{9,8},{10,11... | collective-permute-start | bytes 6152 | tf_op jit(solution)/shard_map/ppermute | solution.py:33
  139.4 3.5 %collective-permute-start.11 = (f32[4,128]{1,0:T(4,128)S(1)}, f32[4,128]{1,0:T(4,128)S(1)}, u32[]{:S(2)}, u32[]{:S(2)}) collective-permute-start(f32[4,128]{1,0:T(4,128)S(1)} %slice.23), channel_id=1, source_target_pairs={{0,1},{1,0},{2,3},{3,2},{4,5},{5,4},{6,7},{7,6},{8,9},{9,8},{10,11... | collective-permute-start | bytes 6152 | tf_op jit(solution)/shard_map/ppermute | solution.py:33

commit v5 on v4

--- a/solution.py
+++ b/solution.py
@@ -164,7 +164,7 @@
                 base += size
     for slot in range(SLOTS):
 
-        @pl.when(ids_ref[0, slot] >= NBLK)
+        @pl.when(ids_ref[0, 0, slot] >= NBLK)
         def _():
             picked_ref[:, slot * BLK : (slot + 1) * BLK] = jnp.zeros((picked_ref.shape[0], BLK), BF16)
 
@@ -305,7 +305,8 @@
     near = jnp.concatenate([near] + [swapped(near, ("py_1", CORE), bits) for bits in (1, 2, 3)])
     plane_ids = [near] + [swapped(near, "py_0", bits) for bits in (1, 2, 3)]
     place = lax.axis_index(PLANE).reshape(1, 1)
-    outgoing = select(stage(place, plane_ids), spread)
+    staged = stage(place, plane_ids)
+    outgoing = select(staged, spread)
     outgoing, plane_ids, my_ids, peer_ids = lax.optimization_barrier(
         (outgoing, plane_ids, my_ids, near[2])
     )
@@ -330,7 +331,7 @@
     tile_movie = pltpu.with_memory_space_constraint(movie.reshape(pixels, frames), pltpu.HBM)
     tile_foot = pltpu.with_memory_space_constraint(footprints.reshape(pixels, WIDTH), pltpu.HBM)
     current, colsq, cross, gram, inv = first_pass(
-        my_ids[None], column_live, received, tile_movie, tile_foot
+        staged, column_live, received, tile_movie, tile_foot
     )
     scale = live[:, None] / jnp.sqrt(totals_of(colsq, match) / pixall + 1e-06)
     current, colsq = second_pass(scale.reshape(1, WIDTH), current, cross, gram, inv)

time: 145 us -> 145 us (level)
  no operation moved by 1% of the time
where the time goes in v5:
time: 145 us
  starting transfers between devices  46.9 us (32%)
  waiting for transfers between devices  39.3 us (27%)
  blocking collectives  37.2 us (26%)
  Pallas kernels  14.8 us (10%)
  local copies, waits for them, and re-layouts  4.2 us (3%)
    all_to_all x2, blocking collectives, to_everyone(): return lax.all_to_all(copies, axes, split_axis=0, concat_axis=0, tiled=True)  37.2 us
    all_to_all x1, waiting for transfers between devices, per_device(): lax.all_to_all(outgoing, PLANE, split_axis=0, concat_axis=0, tiled=True)  27.8 us
    ppermute x12, starting transfers between devices, swapped(): lax.ppermute(value, axis, [(i, i ^ bits) for i in range(lax.axis_size(axi...  23.7 us
    all_to_all x1, starting transfers between devices, per_device(): lax.all_to_all(pieces, COLUMN, split_axis=0, concat_axis=0, tiled=True)  13.5 us
    ppermute x12, waiting for transfers between devices, swapped(): lax.ppermute(value, axis, [(i, i ^ bits) for i in range(lax.axis_size(axi...  11.4 us
    all_to_all x1, starting transfers between devices, per_device(): lax.all_to_all(outgoing, PLANE, split_axis=0, concat_axis=0, tiled=True)  9.69 us
    pallas_call x1, Pallas kernels, first_pass(): pl.pallas_call(first_kernel, out_shape=(pltpu.VMEM((pixels, WIDTH), F32),...  8.07 us
  transfers between devices with their start and end apart: 14, of which 10 were waited for; matrix products, arithmetic and copies ran while one was open for 2% of the time, Pallas kernels for 1%

profile of v5, /device:TPU:1, one launch (start us, length us, event | category | flops | bytes accessed | tf_op | source)
XLA Modules:
  0.0 144.5 jit_solution(18260430939912878567)
XLA Ops:
  0.0 0.0 copy-start
  0.0 1.7 %broadcast_in_dim.9 = bf16[8,8,8,512]{3,2,1,0:T(8,128)(2,1)} broadcast(bf16[8,8,512]{2,1,0:T(8,128)(2,1)} %bitcast.56), dimensions={0,2,3} | broadcast | bytes 589824 | tf_op jit(solution)/shard_map/broadcast_in_dim | solution.py:298
  1.7 13.5 %all-to-all-start = ((bf16[64,8,512]{2,1,0:T(8,128)(2,1)}), bf16[64,8,512]{2,1,0:T(8,128)(2,1)S(1)}, u32[]{:S(2)}, u32[]{:S(2)}) async-start(bf16[64,8,512]{2,1,0:T(8,128)(2,1)} %bitcast.4), calls=%async_computation | async-start | bytes 1048576 | tf_op jit(solution)/shard_map/all_to_all | solution.py:301
  15.2 2.7 %collective-permute-start = (s32[1,4]{1,0:T(1,128)}, s32[1,4]{1,0:T(1,128)S(1)}, u32[]{:S(2)}, u32[]{:S(2)}) collective-permute-start(s32[1,4]{1,0:T(1,128)} %bitcast.58), channel_id=1, source_target_pairs={{0,16},{16,0},{1,17},{17,1},{2,18},{18,2},{3,19},{19,3},{4,20},{20... | collective-permute-start | bytes 56 | tf_op jit(solution)/shard_map/ppermute | solution.py:33
  17.9 1.5 %collective-permute-done = s32[1,4]{1,0:T(1,128)S(1)} collective-permute-done((s32[1,4]{1,0:T(1,128)}, s32[1,4]{1,0:T(1,128)S(1)}, u32[]{:S(2)}, u32[]{:S(2)}) %collective-permute-start) | collective-permute-done | bytes 48 | tf_op jit(solution)/shard_map/ppermute | solution.py:33
  19.4 0.7 pad_add_fusion.1
  20.0 3.2 %collective-permute-start.3 = (s32[2,4]{1,0:T(2,128)S(1)}, s32[2,4]{1,0:T(2,128)S(1)}, u32[]{:S(2)}, u32[]{:S(2)}) collective-permute-start(s32[2,4]{1,0:T(2,128)S(1)} %pad_add_fusion.1), channel_id=1, source_target_pairs={{0,33},{1,32},{32,1},{33,0},{2,35},{3,34},{34,3},{35,2},{4,37},{5,... | collective-permute-start | bytes 104 | tf_op jit(solution)/shard_map/ppermute | solution.py:33
  23.3 0.2 collective-permute-start.2
  23.4 0.3 collective-permute-start.1
  23.8 1.1 collective-permute-done.3
  24.9 1.1 collective-permute-done.2
  26.0 0.0 collective-permute-done.1
  26.0 0.7 concatenate.26.refs_0_
  26.7 2.7 %collective-permute-start.6 = (s32[8,4]{1,0:T(8,128)S(1)}, s32[8,4]{1,0:T(8,128)S(1)}, u32[]{:S(2)}, u32[]{:S(2)}) collective-permute-start(s32[8,4]{1,0:T(8,128)S(1)} %concatenate.26.refs_0_), channel_id=1, source_target_pairs={{0,192},{64,128},{128,64},{192,0},{1,193},{65,129},{129,65},{193,1... | collective-permute-start | bytes 392 | tf_op jit(solution)/shard_map/ppermute | solution.py:33
  29.4 0.4 collective-permute-start.5
  29.8 0.3 collective-permute-start.4
  30.1 0.7 collective-permute-done.6.refs_3_
  30.7 2.9 %collective-permute-done.5.refs_2_ = s32[8,4]{1,0:T(8,128)S(1)} collective-permute-done((s32[8,4]{1,0:T(8,128)S(1)}, s32[8,4]{1,0:T(8,128)S(1)}, u32[]{:S(2)}, u32[]{:S(2)}) %collective-permute-start.5) | collective-permute-done | bytes 160 | tf_op jit(solution)/shard_map/ppermute | solution.py:33
  33.7 0.0 collective-permute-done.4.refs_1_
  33.7 0.8 stage.1.ids_ref
  34.5 0.0 all-to-all-done.rows_ref
  34.5 1.8 %select.1 = bf16[32,4,8,8,128]{4,3,2,1,0:T(8,128)(2,1)} custom-call(s32[5,8,4]{2,1,0:T(8,128)S(4)} %stage.1.ids_ref, bf16[64,8,512]{2,1,0:T(8,128)(2,1)S(1)} %all-to-all-done.rows_ref), custom_call_target="tpu_custom_call" | custom-call | flops 1048576 | bytes 4194304 | tf_op jit(solution)/shard_map/select/pallas_call | solution.py:99
  36.3 0.1 copy.35
  36.4 0.1 copy.36
  36.4 0.1 copy.37
  36.5 0.1 copy.38
  36.6 0.1 pad_add_fusion
  36.7 1.2 collective-permute-start.7
  37.9 1.2 collective-permute-done.7
  39.1 0.1 concatenate.29
  39.2 2.1 %collective-permute-start.8 = (s32[64,4]{0,1:T(4,128)S(1)}, s32[64,4]{0,1:T(4,128)S(1)}, u32[]{:S(2)}, u32[]{:S(2)}) collective-permute-start(s32[64,4]{0,1:T(4,128)S(1)} %concatenate.29), channel_id=1, source_target_pairs={{0,4},{2,6},{4,0},{6,2},{8,12},{10,14},{12,8},{14,10},{1,5},{3,7},... | collective-permute-start | bytes 3080 | tf_op jit(solution)/shard_map/ppermute | solution.py:33
  41.3 0.0 copy-done
  41.3 1.2 collective-permute-done.8
  42.6 0.1 concatenate.30
  42.7 4.8 %collective-permute-start.9 = (s32[128,4]{0,1:T(4,128)S(1)}, s32[128,4]{0,1:T(4,128)S(1)}, u32[]{:S(2)}, u32[]{:S(2)}) collective-permute-start(s32[128,4]{0,1:T(4,128)S(1)} %concatenate.30), channel_id=1, source_target_pairs={{0,8},{2,10},{4,12},{6,14},{8,0},{10,2},{12,4},{14,6},{1,9},{3,11}... | collective-permute-start | bytes 6152 | tf_op jit(solution)/shard_map/ppermute | solution.py:33
  47.5 0.1 pad_add_fusion.2
  47.6 9.7 %all-to-all-start.1 = ((bf16[32,4,8,8,128]{4,3,2,1,0:T(8,128)(2,1)}), bf16[32,4,8,8,128]{4,3,2,1,0:T(8,128)(2,1)S(1)}, u32[]{:S(2)}, u32[]{:S(2)}) async-start(bf16[32,4,8,8,128]{4,3,2,1,0:T(8,128)(2,1)} %select.1), calls=%async_computation.1 | async-start | bytes 4194304 | tf_op jit(solution)/shard_map/all_to_all | solution.py:314
  57.3 0.0 collective-permute-done.9
  57.3 0.1 concatenate.31
  57.4 0.1 copy.39
  57.6 0.2 reshape.90
  58.2 0.1 eq.16
  58.3 0.1 compare_convert_fusion
  58.4 0.7 div.20
  59.0 27.8 %all-to-all-done.1 = bf16[32,4,8,8,128]{4,3,2,1,0:T(8,128)(2,1)S(1)} async-done(((bf16[32,4,8,8,128]{4,3,2,1,0:T(8,128)(2,1)}), bf16[32,4,8,8,128]{4,3,2,1,0:T(8,128)(2,1)S(1)}, u32[]{:S(2)}, u32[]{:S(2)}) %all-to-all-start.1) | async-done | bytes 2097184 | tf_op jit(solution)/shard_map/all_to_all | solution.py:314
  86.9 8.1 %first_pass.1 = (f32[1024,512]{1,0:T(8,128)S(1)}, f32[4,128]{1,0:T(4,128)S(1)}, f32[1024,512]{1,0:T(8,128)S(1)}, bf16[4,512,256]{2,1,0:T(8,128)(2,1)S(1)}, f32[1,512]{1,0:T(1,128)S(1)}) custom-call(s32[5,8,4]{2,1,0:T(8,128)S(4)} %stage.1.ids_ref, f32[1,512]{1,0:T(1,128)} %bitcast.57, bf16[8,2,2,4,8,8,128]{6,5,4,3,2,1,0:T(8,128)(2,1)S(1)} %bitcast.42, ...), custom_call_target="tpu_custom_call" | custom-call | flops 7516192768 | bytes 12582912 | tf_op jit(solution)/shard_map/first_pass/pallas_call | solution.py:230
  95.0 18.5 %all_to_all.20 = f32[128,4,128]{2,1,0:T(4,128)S(1)} all-to-all(f32[128,4,128]{2,1,0:T(4,128)S(1)} %broadcast_in_dim.10), channel_id=1, replica_groups=mesh['py_0'=4,'py_1'=2,'px_0'=2,'px_1'=8,'px_2'=2] {'px_0','py_1','px_1'..., dimensions={0} | all-to-all | bytes 524288 | tf_op jit(solution)/shard_map/all_to_all | solution.py:29
  113.5 0.2 fusion
  113.7 3.0 %collective-permute-start.10 = (f32[4,128]{1,0:T(4,128)S(1)}, f32[4,128]{1,0:T(4,128)S(1)}, u32[]{:S(2)}, u32[]{:S(2)}) collective-permute-start(f32[4,128]{1,0:T(4,128)S(1)} %slice.21), channel_id=1, source_target_pairs={{0,1},{1,0},{2,3},{3,2},{4,5},{5,4},{6,7},{7,6},{8,9},{9,8},{10,11... | collective-permute-start | bytes 6152 | tf_op jit(solution)/shard_map/ppermute | solution.py:33
  116.8 0.8 collective-permute-done.10
  117.6 0.1 rsqrt_multiply_fusion.1
  117.7 2.7 %second_pass.1 = (f32[1024,512]{1,0:T(8,128)S(1)}, f32[4,128]{1,0:T(4,128)S(1)}) custom-call(f32[1,512]{1,0:T(1,128)S(1)} %bitcast.44, f32[1024,512]{1,0:T(8,128)S(1)} %get-tuple-element.31.old_ref, f32[1024,512]{1,0:T(8,128)S(1)} %get-tuple-element.32.cross_ref, bf16[4,512,256]{2,1,0:T(8,128)(2,1)S(1)} %get-tuple-element.33.gram_ref, ...), custom_call_target="tpu_custom_call" | custom-call | flops 4294967296 | bytes 8388608 | tf_op jit(solution)/shard_map/second_pass/pallas_call | solution.py:258
  120.5 18.7 %all_to_all.21 = f32[128,4,128]{2,1,0:T(4,128)S(1)} all-to-all(f32[128,4,128]{2,1,0:T(4,128)S(1)} %broadcast_in_dim.11), channel_id=1, replica_groups=mesh['py_0'=4,'py_1'=2,'px_0'=2,'px_1'=8,'px_2'=2] {'px_0','py_1','px_1'..., dimensions={0} | all-to-all | bytes 524288 | tf_op jit(solution)/shard_map/all_to_all | solution.py:29
  139.2 0.2 fusion.1
  139.4 2.7 %collective-permute-start.11 = (f32[4,128]{1,0:T(4,128)S(1)}, f32[4,128]{1,0:T(4,128)S(1)}, u32[]{:S(2)}, u32[]{:S(2)}) collective-permute-start(f32[4,128]{1,0:T(4,128)S(1)} %slice.23), channel_id=1, source_target_pairs={{0,1},{1,0},{2,3},{3,2},{4,5},{5,4},{6,7},{7,6},{8,9},{9,8},{10,11... | collective-permute-start | bytes 6152 | tf_op jit(solution)/shard_map/ppermute | solution.py:33
  142.1 0.8 collective-permute-done.11
  142.9 0.1 rsqrt_multiply_fusion
  143.0 1.4 last_scaling.1
  (20 shorter events, 0.5 us)
Async XLA Ops:
  0.0 41.3 %copy-start = (s32[1,1,4]{2,1,0:T(1,128)S(1)}, s32[1,1,4]{2,1,0:T(1,128)}, u32[]{:S(2)}) copy-start(s32[1,1,4]{2,1,0:T(1,128)} %param.7) | copy-start | bytes 52
  1.7 32.8 %all-to-all-start = ((bf16[64,8,512]{2,1,0:T(8,128)(2,1)}), bf16[64,8,512]{2,1,0:T(8,128)(2,1)S(1)}, u32[]{:S(2)}, u32[]{:S(2)}) async-start(bf16[64,8,512]{2,1,0:T(8,128)(2,1)} %bitcast.4), calls=%async_computation | async-start | bytes 1048576 | tf_op jit(solution)/shard_map/all_to_all | solution.py:301
  15.2 4.2 %collective-permute-start = (s32[1,4]{1,0:T(1,128)}, s32[1,4]{1,0:T(1,128)S(1)}, u32[]{:S(2)}, u32[]{:S(2)}) collective-permute-start(s32[1,4]{1,0:T(1,128)} %bitcast.58), channel_id=1, source_target_pairs={{0,16},{16,0},{1,17},{17,1},{2,18},{18,2},{3,19},{19,3},{4,20},{20... | collective-permute-start | bytes 56 | tf_op jit(solution)/shard_map/ppermute | solution.py:33
  20.0 4.8 %collective-permute-start.3 = (s32[2,4]{1,0:T(2,128)S(1)}, s32[2,4]{1,0:T(2,128)S(1)}, u32[]{:S(2)}, u32[]{:S(2)}) collective-permute-start(s32[2,4]{1,0:T(2,128)S(1)} %pad_add_fusion.1), channel_id=1, source_target_pairs={{0,33},{1,32},{32,1},{33,0},{2,35},{3,34},{34,3},{35,2},{4,37},{5,... | collective-permute-start | bytes 104 | tf_op jit(solution)/shard_map/ppermute | solution.py:33
  23.3 2.7 %collective-permute-start.2 = (s32[2,4]{1,0:T(2,128)S(1)}, s32[2,4]{1,0:T(2,128)S(1)}, u32[]{:S(2)}, u32[]{:S(2)}) collective-permute-start(s32[2,4]{1,0:T(2,128)S(1)} %pad_add_fusion.1), channel_id=1, source_target_pairs={{0,32},{1,33},{32,0},{33,1},{2,34},{3,35},{34,2},{35,3},{4,36},{5,... | collective-permute-start | bytes 104 | tf_op jit(solution)/shard_map/ppermute | solution.py:33
  23.4 2.6 %collective-permute-start.1 = (s32[2,4]{1,0:T(2,128)S(1)}, s32[2,4]{1,0:T(2,128)S(1)}, u32[]{:S(2)}, u32[]{:S(2)}) collective-permute-start(s32[2,4]{1,0:T(2,128)S(1)} %pad_add_fusion.1), channel_id=1, source_target_pairs={{0,1},{1,0},{32,33},{33,32},{2,3},{3,2},{34,35},{35,34},{4,5},{5,4... | collective-permute-start | bytes 104 | tf_op jit(solution)/shard_map/ppermute | solution.py:33
  26.7 4.1 %collective-permute-start.6 = (s32[8,4]{1,0:T(8,128)S(1)}, s32[8,4]{1,0:T(8,128)S(1)}, u32[]{:S(2)}, u32[]{:S(2)}) collective-permute-start(s32[8,4]{1,0:T(8,128)S(1)} %concatenate.26.refs_0_), channel_id=1, source_target_pairs={{0,192},{64,128},{128,64},{192,0},{1,193},{65,129},{129,65},{193,1... | collective-permute-start | bytes 392 | tf_op jit(solution)/shard_map/ppermute | solution.py:33
  29.4 4.3 %collective-permute-start.5 = (s32[8,4]{1,0:T(8,128)S(1)}, s32[8,4]{1,0:T(8,128)S(1)}, u32[]{:S(2)}, u32[]{:S(2)}) collective-permute-start(s32[8,4]{1,0:T(8,128)S(1)} %concatenate.26.refs_0_), channel_id=1, source_target_pairs={{0,128},{64,192},{128,0},{192,64},{1,129},{65,193},{129,1},{193,65... | collective-permute-start | bytes 392 | tf_op jit(solution)/shard_map/ppermute | solution.py:33
  29.8 3.9 %collective-permute-start.4 = (s32[8,4]{1,0:T(8,128)S(1)}, s32[8,4]{1,0:T(8,128)S(1)}, u32[]{:S(2)}, u32[]{:S(2)}) collective-permute-start(s32[8,4]{1,0:T(8,128)S(1)} %concatenate.26.refs_0_), channel_id=1, source_target_pairs={{0,64},{64,0},{128,192},{192,128},{1,65},{65,1},{129,193},{193,129... | collective-permute-start | bytes 392 | tf_op jit(solution)/shard_map/ppermute | solution.py:33
  36.7 2.5 %collective-permute-start.7 = (s32[32,4]{0,1:T(4,128)S(1)}, s32[32,4]{0,1:T(4,128)S(1)}, u32[]{:S(2)}, u32[]{:S(2)}) collective-permute-start(s32[32,4]{0,1:T(4,128)S(1)} %pad_add_fusion), channel_id=1, source_target_pairs={{0,2},{2,0},{4,6},{6,4},{8,10},{10,8},{12,14},{14,12},{1,3},{3,1},... | collective-permute-start | bytes 1544 | tf_op jit(solution)/shard_map/ppermute | solution.py:33
  39.2 3.3 %collective-permute-start.8 = (s32[64,4]{0,1:T(4,128)S(1)}, s32[64,4]{0,1:T(4,128)S(1)}, u32[]{:S(2)}, u32[]{:S(2)}) collective-permute-start(s32[64,4]{0,1:T(4,128)S(1)} %concatenate.29), channel_id=1, source_target_pairs={{0,4},{2,6},{4,0},{6,2},{8,12},{10,14},{12,8},{14,10},{1,5},{3,7},... | collective-permute-start | bytes 3080 | tf_op jit(solution)/shard_map/ppermute | solution.py:33
  42.7 14.6 %collective-permute-start.9 = (s32[128,4]{0,1:T(4,128)S(1)}, s32[128,4]{0,1:T(4,128)S(1)}, u32[]{:S(2)}, u32[]{:S(2)}) collective-permute-start(s32[128,4]{0,1:T(4,128)S(1)} %concatenate.30), channel_id=1, source_target_pairs={{0,8},{2,10},{4,12},{6,14},{8,0},{10,2},{12,4},{14,6},{1,9},{3,11}... | collective-permute-start | bytes 6152 | tf_op jit(solution)/shard_map/ppermute | solution.py:33
  47.6 39.3 %all-to-all-start.1 = ((bf16[32,4,8,8,128]{4,3,2,1,0:T(8,128)(2,1)}), bf16[32,4,8,8,128]{4,3,2,1,0:T(8,128)(2,1)S(1)}, u32[]{:S(2)}, u32[]{:S(2)}) async-start(bf16[32,4,8,8,128]{4,3,2,1,0:T(8,128)(2,1)} %select.1), calls=%async_computation.1 | async-start | bytes 4194304 | tf_op jit(solution)/shard_map/all_to_all | solution.py:314
  113.7 3.9 %collective-permute-start.10 = (f32[4,128]{1,0:T(4,128)S(1)}, f32[4,128]{1,0:T(4,128)S(1)}, u32[]{:S(2)}, u32[]{:S(2)}) collective-permute-start(f32[4,128]{1,0:T(4,128)S(1)} %slice.21), channel_id=1, source_target_pairs={{0,1},{1,0},{2,3},{3,2},{4,5},{5,4},{6,7},{7,6},{8,9},{9,8},{10,11... | collective-permute-start | bytes 6152 | tf_op jit(solution)/shard_map/ppermute | solution.py:33
  139.4 3.5 %collective-permute-start.11 = (f32[4,128]{1,0:T(4,128)S(1)}, f32[4,128]{1,0:T(4,128)S(1)}, u32[]{:S(2)}, u32[]{:S(2)}) collective-permute-start(f32[4,128]{1,0:T(4,128)S(1)} %slice.23), channel_id=1, source_target_pairs={{0,1},{1,0},{2,3},{3,2},{4,5},{5,4},{6,7},{7,6},{8,9},{9,8},{10,11... | collective-permute-start | bytes 6152 | tf_op jit(solution)/shard_map/ppermute | solution.py:33
